TPU v7x, 256 devices: a whole 4x4x8 slice. The times are simulated.
256 devices in a mesh: blk: 16 (over x, y_hi, core), grp: 16 (over y_lo, z).
Axes of the slice: x: 4, y: 4 (y_hi: 2, y_lo: 2; y = y_hi * 2 + y_lo), z: 8, core: 2. Of those that a mesh axis runs over, the one named last changes fastest.
Arguments:
- amplitudes: bfloat16 [896, 4, 896], P('blk', None, 'grp'), may hold values from -6 to 6
- grid_factor: bfloat16 [8192, 896], P(('blk', 'grp')), may hold values from -0.1875 to 0.1875
- metric: float32 [8192, 16, 512], P('blk', 'grp'), may hold values from -0.625 to 0.625
- virt_energy: float32 [896], replicated, may hold values from 0.2 to 4
- pair_energy: float32 [4], replicated, may hold values from -2 to -0.5
Outputs:
- residual: float32 [896, 4, 896], P('blk', None, 'grp')
All inputs are finite; a program needn't handle non-finite values.
Results may differ from a plain program's by a relative error of at most 0.005.
Values may be sent and summed in bfloat16 or wider, within the bound.
A program may use at most 64 MiB of HBM per device.

v0:
```python
import jax
import jax.numpy as jnp
from jax import lax
from jax.sharding import Mesh
from jax.sharding import PartitionSpec as P

GRP = ("grp_0", "grp_1")
BLK_GRP = ("blk", "grp_0", "grp_1")


def from_everyone(x, axis):
    count = lax.axis_size(axis)
    return lax.all_to_all(jnp.broadcast_to(x[None], (count, *x.shape)), axis, 0, 0, tiled=True)


def joined_along(pieces, dim):
    shape = list(pieces.shape[1:])
    shape[dim] *= pieces.shape[0]
    return jnp.moveaxis(pieces, 0, dim).reshape(shape)


def gather_directly(x, axis, dim):
    pieces = from_everyone(x, axis)
    return joined_along(pieces, dim)


def stacked_from(x, axes, sequence):
    pieces = x[None]
    for k in sequence:
        pieces = lax.all_gather(pieces, axes[k], axis=0, tiled=True)
    current = [lax.axis_size(axes[k]) for k in reversed(sequence)]
    pieces = pieces.reshape(*current, *x.shape)
    turned = sorted(range(len(sequence)), key=lambda place: sequence[len(sequence) - 1 - place])
    return pieces.transpose(*turned, *range(len(sequence), pieces.ndim)).reshape(-1, *x.shape)


def gather_axes(x, axes, sequence, dim):
    return joined_along(stacked_from(x, axes, sequence), dim)


def own_block(pieces, axes, sequence):
    shape = [lax.axis_size(a) for a in axes]
    pieces = pieces.reshape(*shape, *pieces.shape[1:])
    pieces = pieces.transpose(*sequence, *range(len(axes), pieces.ndim))
    pieces = pieces.reshape(-1, *pieces.shape[len(axes) :])
    for k in sequence:
        pieces = lax.psum_scatter(pieces, axes[k], scatter_dimension=0, tiled=True)
    return pieces[0]


def cut_along(x, dim, count):
    shape = x.shape
    pieces = x.reshape(*shape[:dim], count, shape[dim] // count, *shape[dim + 1 :])
    return jnp.moveaxis(pieces, dim, 0)


def sum_by_axis(x, axes, sequence, dim):
    count = lax.axis_size(axes)
    return own_block(cut_along(x, dim, count), axes, sequence)


def sent_and_summed(x, axis, dim):
    pieces = cut_along(x, dim, lax.axis_size(axis))
    arrived = lax.all_to_all(pieces, axis, split_axis=0, concat_axis=0, tiled=True)
    return arrived.astype(jnp.float32).sum(axis=0)


def local(amplitudes, grid_factor, metric, virt_energy, pair_energy):
    row_factor = gather_directly(grid_factor, GRP, 0)
    column_factor = gather_directly(grid_factor, "blk", 0)
    amplitude_rows = gather_directly(amplitudes, "blk", 0)
    row_count = row_factor.shape[0]
    left_part = jnp.einsum(
        "pc,ckd->kpd", row_factor, amplitude_rows, preferred_element_type=jnp.float32
    ).astype(jnp.bfloat16)
    columns = column_factor
    products = jnp.einsum(
        "kpd,qd->kpq",
        gather_axes(left_part, GRP, (0, 1), 2),
        columns,
        preferred_element_type=jnp.float32,
    )
    weighted = (metric.reshape(row_count, -1)[None] * products).astype(jnp.bfloat16)
    columns = column_factor
    mixed = (
        sum_by_axis(
            jnp.einsum("kpq,qb->bkp", weighted, columns, preferred_element_type=jnp.float32).astype(
                jnp.bfloat16
            ),
            GRP,
            (1, 0),
            0,
        )
        .astype(jnp.float32)
        .astype(jnp.bfloat16)
    )
    columns = row_factor
    ladder = sent_and_summed(
        jnp.einsum("pa,bkp->akb", columns, mixed, preferred_element_type=jnp.float32).astype(
            jnp.bfloat16
        ),
        "blk",
        0,
    )
    first_energy = lax.dynamic_slice_in_dim(
        virt_energy, lax.axis_index("blk") * amplitudes.shape[0], amplitudes.shape[0]
    )
    second_energy = lax.dynamic_slice_in_dim(
        virt_energy, lax.axis_index(GRP) * amplitudes.shape[2], amplitudes.shape[2]
    )
    denominator = (
        first_energy[:, None, None] + second_energy[None, None, :] - pair_energy[None, :, None]
    )
    return denominator * amplitudes.astype(jnp.float32) + ladder


def solution(mesh):
    split = Mesh(mesh.devices.reshape(mesh.shape["blk"], 2, 8), ("blk", "grp_0", "grp_1"))
    in_specs = (P("blk", None, GRP), P(BLK_GRP, None), P("blk", GRP, None), P(), P())
    out_specs = P("blk", None, GRP)
    return jax.shard_map(local, mesh=split, in_specs=in_specs, out_specs=out_specs, check_vma=False)
```

profile of v0, /device:TPU:1, one launch (start us, length us, event | category | flops | bytes accessed | tf_op | source)
XLA Modules:
  0.0 239.4 jit_solution(6617497980471759122)
XLA Ops:
  6.5 0.9 copy.17
  7.5 0.1 broadcast_bitcast_fusion
  7.6 1.5 reshape.67
  9.1 18.4 %all_to_all.20 = bf16[16,2,6272]{2,1,0:T(2,128)(2,1)S(1)} all-to-all(bf16[16,2,6272]{2,1,0:T(2,128)(2,1)S(1)} %reshape.67), channel_id=1, replica_groups=mesh['blk'=16,'grp_0'=2,'grp_1'=8] {'blk'}, dimensions={0} | all-to-all | bytes 802816 | tf_op jit(solution)/shard_map/all_to_all | solution.py:13
  27.5 1.8 broadcast_in_dim.7
  29.3 8.4 %all-to-all-start.1 = ((bf16[16,32,896]{2,1,0:T(8,128)(2,1)}), bf16[16,32,896]{2,1,0:T(8,128)(2,1)S(1)}, u32[]{:S(2)}, u32[]{:S(2)}) async-start(bf16[16,32,896]{2,1,0:T(8,128)(2,1)} %broadcast_in_dim.7), calls=%async_computation.1 | async-start | bytes 1835008 | tf_op jit(solution)/shard_map/all_to_all | solution.py:13
  37.8 1.6 reshape.68
  39.4 0.4 copy.19
  39.8 1.1 reshape.56
  40.9 19.1 %all-to-all-done.1 = bf16[16,32,896]{2,1,0:T(8,128)(2,1)S(1)} async-done(((bf16[16,32,896]{2,1,0:T(8,128)(2,1)}), bf16[16,32,896]{2,1,0:T(8,128)(2,1)S(1)}, u32[]{:S(2)}, u32[]{:S(2)}) %all-to-all-start.1) | async-done | bytes 917536 | tf_op jit(solution)/shard_map/all_to_all | solution.py:13
  60.0 0.5 fusion.1
  60.4 5.6 %all-gather = bf16[8,512,56]{1,2,0:T(8,128)(2,1)} all-gather(bf16[4,512,56]{1,2,0:T(8,128)(2,1)S(1)} %fusion.1), channel_id=2, replica_groups=mesh['blk'=16,'grp_0'=2,'grp_1'=8] {'grp_0'}, dimensions={0}, use_global_device_ids=true | all-gather | bytes 688128 | tf_op jit(solution)/shard_map/all_gather | solution.py:30
  66.1 7.9 %all-to-all-start.2 = ((bf16[16,32,896]{2,1,0:T(8,128)(2,1)}), bf16[16,32,896]{2,1,0:T(8,128)(2,1)S(1)}, u32[]{:S(2)}, u32[]{:S(2)}) async-start(bf16[16,32,896]{2,1,0:T(8,128)(2,1)} %broadcast_in_dim.7), calls=%async_computation.2 | async-start | bytes 1835008 | tf_op jit(solution)/shard_map/all_to_all | solution.py:13
  74.0 1.3 copy.33
  75.3 40.1 %all-gather.3.cloned.1.call-done = bf16[16,4,512,56]{2,3,1,0:T(8,128)(2,1)} async-done(((bf16[2,4,512,56]{2,3,1,0:T(8,128)(2,1)}), bf16[16,4,512,56]{2,3,1,0:T(8,128)(2,1)}) %all-gather.3.cloned.1.call-update) | async-done | bytes 3670032 | tf_op jit(solution)/shard_map/all_gather | solution.py:30
  115.5 2.3 copy.20
  117.8 2.1 copy.21
  119.8 7.5 %convert_bitcast_fusion = bf16[896,4,512]{0,2,1:T(8,128)(2,1)} fusion(bf16[512,896,1]{1,0,2:T(8,128)(2,1)S(1)} %bitcast.61, bf16[4,512,896]{1,2,0:T(8,128)(2,1)} %bitcast.56, f32[512,512]{1,0:T(8,128)S(1)} %bitcast.60), kind=kOutput, calls=%fused_computation.1 | convolution fusion | flops 3762028544 | bytes 9306112 | tf_op jit(solution)/shard_map/kpq,qb->bkp/dot_general | solution.py:87
  127.4 5.9 %copy.23 = bf16[896,4,512]{2,0,1:T(8,128)(2,1)} copy(bf16[896,4,512]{0,2,1:T(8,128)(2,1)} %convert_bitcast_fusion) | data formatting | bytes 7340032 | tf_op jit(solution)/shard_map/convert_element_type | solution.py:87
  133.3 4.3 %copy.24 = bf16[8,2,56,4,512]{4,2,3,1,0:T(8,128)(2,1)} copy(bf16[8,2,56,4,512]{4,2,0,1,3:T(8,128)(2,1)} %bitcast.52) | data formatting | bytes 7340032 | tf_op jit(solution)/shard_map/transpose | solution.py:44
  137.7 49.2 %reduce-scatter.3.cloned.1.call-done = bf16[2,56,4,512]{3,1,2,0:T(8,128)(2,1)} async-done(((bf16[16,56,4,512]{3,1,2,0:T(8,128)(2,1)}), bf16[2,56,4,512]{3,1,2,0:T(8,128)(2,1)}) %reduce-scatter.3.cloned.1.call-update) | async-done | bytes 458768 | tf_op jit(solution)/shard_map/reduce_scatter | solution.py:47
  186.9 20.5 %reduce-scatter.5.cloned.1.call-done = bf16[1,56,4,512]{3,1,2,0:T(8,128)(2,1)} async-done(((bf16[2,56,4,512]{3,1,2,0:T(8,128)(2,1)}), bf16[1,56,4,512]{3,1,2,0:T(8,128)(2,1)}) %reduce-scatter.5.cloned.1.call-update) | async-done | bytes 229392 | tf_op jit(solution)/shard_map/reduce_scatter | solution.py:47
  207.4 1.4 fusion
  208.8 1.5 reshape.63
  210.3 0.2 copy.34
  210.5 2.2 reshape.69
  212.7 7.2 %all-to-all-start.3 = ((bf16[16,2,6272]{2,1,0:T(2,128)(2,1)}), bf16[16,2,6272]{2,1,0:T(2,128)(2,1)S(1)}, u32[]{:S(2)}, u32[]{:S(2)}) async-start(bf16[16,2,6272]{2,1,0:T(2,128)(2,1)} %reshape.69), calls=%async_computation.5 | async-start | bytes 802816 | tf_op jit(solution)/shard_map/all_to_all | solution.py:64
  220.0 0.8 fusion.3
  220.9 9.3 %all-to-all-done.3 = bf16[16,2,6272]{2,1,0:T(2,128)(2,1)S(1)} async-done(((bf16[16,2,6272]{2,1,0:T(2,128)(2,1)}), bf16[16,2,6272]{2,1,0:T(2,128)(2,1)S(1)}, u32[]{:S(2)}, u32[]{:S(2)}) %all-to-all-start.3) | async-done | bytes 401440 | tf_op jit(solution)/shard_map/all_to_all | solution.py:64
  230.2 1.6 reshape.70
  231.8 0.2 convert_reduce_fusion
  232.1 0.7 copy.27
  (11 shorter events, 0.3 us)
Async XLA Ops:
  29.3 30.7 %all-to-all-start.1 = ((bf16[16,32,896]{2,1,0:T(8,128)(2,1)}), bf16[16,32,896]{2,1,0:T(8,128)(2,1)S(1)}, u32[]{:S(2)}, u32[]{:S(2)}) async-start(bf16[16,32,896]{2,1,0:T(8,128)(2,1)} %broadcast_in_dim.7), calls=%async_computation.1 | async-start | bytes 1835008 | tf_op jit(solution)/shard_map/all_to_all | solution.py:13
  37.7 77.8 %all-gather.3.cloned.1.call-start = ((), (), s32[]{:S(2)}) async-start(), calls=%async_computation.6 | async-start | bytes 4128768 | tf_op jit(solution)/shard_map/all_gather | solution.py:30
  66.1 53.7 %all-to-all-start.2 = ((bf16[16,32,896]{2,1,0:T(8,128)(2,1)}), bf16[16,32,896]{2,1,0:T(8,128)(2,1)S(1)}, u32[]{:S(2)}, u32[]{:S(2)}) async-start(bf16[16,32,896]{2,1,0:T(8,128)(2,1)} %broadcast_in_dim.7), calls=%async_computation.2 | async-start | bytes 1835008 | tf_op jit(solution)/shard_map/all_to_all | solution.py:13
  74.0 112.9 %reduce-scatter.3.cloned.1.call-start = ((), (), s32[]{:S(2)}) async-start(), calls=%async_computation.7 | async-start | bytes 4128768 | tf_op jit(solution)/shard_map/reduce_scatter | solution.py:47
  137.7 69.8 %reduce-scatter.5.cloned.1.call-start = ((), (), s32[]{:S(2)}) async-start(), calls=%async_computation.8 | async-start | bytes 688128 | tf_op jit(solution)/shard_map/reduce_scatter | solution.py:47
  208.8 23.2 %copy-start = (f32[4]{0:T(128)S(1)}, f32[4]{0:T(128)}, u32[]{:S(2)}) copy-start(f32[4]{0:T(128)} %param.9) | copy-start | bytes 52
  212.7 17.4 %all-to-all-start.3 = ((bf16[16,2,6272]{2,1,0:T(2,128)(2,1)}), bf16[16,2,6272]{2,1,0:T(2,128)(2,1)S(1)}, u32[]{:S(2)}, u32[]{:S(2)}) async-start(bf16[16,2,6272]{2,1,0:T(2,128)(2,1)} %reshape.69), calls=%async_computation.5 | async-start | bytes 802816 | tf_op jit(solution)/shard_map/all_to_all | solution.py:64
Sparse Core Ops, SparseCore 0:
  66.2 49.2 all-gather.2
  137.8 49.0 reduce-scatter.2
  189.4 17.9 reduce-scatter.4
where the time goes:
time: 240 us; the launch traced here: 239 us
  waiting for transfers between devices  138 us (58%)
  local copies, waits for them, and re-layouts  30.5 us (13%)
  blocking collectives  24 us (10%)
  starting transfers between devices  23.7 us (10%)
  between operations  13.2 us (6%)
  matrix products  9.37 us (4%)
    reduce_scatter x2, waiting for transfers between devices, own_block(): pieces = lax.psum_scatter(pieces, axes[k], scatter_dimension=0, tiled=True)  69.7 us
    all_gather x1, waiting for transfers between devices, stacked_from(): pieces = lax.all_gather(pieces, axes[k], axis=0, tiled=True)  40.1 us
    all_to_all x2, waiting for transfers between devices, from_everyone(): lax.all_to_all(jnp.broadcast_to(x[None], (count, *x.shape)), axis, 0, 0,...  19.1 us
    all_to_all x1, blocking collectives, from_everyone(): lax.all_to_all(jnp.broadcast_to(x[None], (count, *x.shape)), axis, 0, 0,...  18.4 us
    all_to_all x2, starting transfers between devices, from_everyone(): lax.all_to_all(jnp.broadcast_to(x[None], (count, *x.shape)), axis, 0, 0,...  16.3 us
    unnamed x9, local copies, waits for them, and re-layouts  9.32 us
    all_to_all x1, waiting for transfers between devices, sent_and_summed(): lax.all_to_all(pieces, axis, split_axis=0, concat_axis=0, tiled=True)  9.27 us
    dot_general x1, matrix products, local(): jnp.einsum('kpq,qb->bkp', weighted, columns, preferred_element_type=jnp.f...  7.54 us
  transfers between devices with their start and end apart: 6, of which 5 were waited for; matrix products, arithmetic and copies ran while one was open for 4% of the time, Pallas kernels for 0%

commit v1 on v0

v1 whole, which is shorter than its diff:
```python
import functools

import jax
import jax.numpy as jnp
from jax import lax
from jax.experimental import pallas as pl
from jax.experimental.pallas import tpu as pltpu
from jax.sharding import PartitionSpec as P

MESH = pl.DeviceIdType.MESH
F32 = jnp.float32
BF16 = jnp.bfloat16
SEMS = 160


class Links:
    def __init__(self, send, recv):
        self.send, self.recv, self.ids, self.open = send, recv, {}, []

    def index(self, key):
        return self.ids.setdefault(key, len(self.ids))

    def copy(self, key, src, dst, dev):
        i = self.index(key)
        return pltpu.make_async_remote_copy(
            src_ref=src, dst_ref=dst, send_sem=self.send.at[i], recv_sem=self.recv.at[i],
            device_id=dev, device_id_type=MESH,
        )

    def start(self, key, src, dst, dev):
        c = self.copy(key, src, dst, dev)
        c.start()
        self.open.append(c)

    def arrived(self, key, dst, dev):
        self.copy(key, dst, dst, dev).wait_recv()

    def close(self):
        for c in self.open:
            c.wait_send()


def kernel(
    tt_ref, x_ref, z_hbm, out_ref,
    tsw, town, tall, xq, xqt, xp, xpt, zb, right, w, mp,
    e1s, e1r, e2s, e2r, eys, eyr, lad, fs, fr, fins, finr,
    send, recv, zsem,
):
    b, g = lax.axis_index("blk"), lax.axis_index("grp")
    core, yh, x = b % 2, (b // 2) % 2, b // 4
    yl, z = g // 8, g % 8
    m = x * 2 + yh
    net = Links(send, recv)

    mate = {"blk": b + 1 - 2 * core, "grp": g}
    xn = {"blk": ((x + 1) % 4) * 4 + b % 4, "grp": g}
    xv = {"blk": ((x + 3) % 4) * 4 + b % 4, "grp": g}
    yp = {"blk": b + 2 - 4 * yh, "grp": g}
    zn = {"blk": b, "grp": yl * 8 + (z + 1) % 8}
    zv = {"blk": b, "grp": yl * 8 + (z + 7) % 8}
    yn = {"blk": b, "grp": (1 - yl) * 8 + z}

    def peer(r):
        return {"blk": b, "grp": (g + r) % 16}

    zcopy = pltpu.make_async_copy(z_hbm.at[:, 0, :], zb.at[core], zsem)
    zcopy.start()

    barrier = pltpu.get_barrier_semaphore()
    near = [mate, xn, xv, yp] + [peer(r) for r in range(1, 16)]
    for dev in near:
        pl.semaphore_signal(barrier, inc=1, device_id=dev, device_id_type=MESH)
    pl.semaphore_wait(barrier, len(near))

    net.start("tsw", tt_ref.at[pl.ds(2 * (1 - core), 2)], tsw, mate)
    net.start("xqy", x_ref, xq.at[m, core], yp)
    net.start("xqn0", x_ref, xq.at[m, core], xn)
    net.start("xqv0", x_ref, xq.at[m, core], xv)
    xq[m, core] = x_ref[...]
    xp[core, g] = x_ref[...]

    net.arrived("tsw", tsw, mate)
    for k in range(2):
        mine = (tt_ref[2 * core + k].astype(F32) + tsw[k].astype(F32)).astype(BF16)
        town[k] = mine
        tall[k, g] = mine
    for k in range(2):
        for r in range(1, 16):
            net.start(("t", k, r), town.at[k], tall.at[k, g], peer(r))

    net.start("zsw", z_hbm.at[:, 0, :], zb.at[core], mate)
    net.start("xpy", x_ref, xp.at[core, g], yn)
    net.start(("xpn", 0, 1), x_ref, xp.at[core, g], zn)
    net.start(("xpv", 0, 1), x_ref, xp.at[core, g], zv)

    my = x * 2 + 1 - yh
    net.arrived("xqy", xq.at[my, core], yp)
    net.start("xqn1", xq.at[my, core], xq.at[my, core], xn)
    net.start("xqv1", xq.at[my, core], xq.at[my, core], xv)
    xm1, xp1, xp2 = (x + 3) % 4, (x + 1) % 4, (x + 2) % 4

    def at_y(o):
        return 1 - yh if o == 1 else yh

    def xqs(xx, o):
        return xq.at[xx * 2 + at_y(o), core]

    net.arrived("xqn0", xqs(xm1, 0), xv)
    net.start("xqf0", xqs(xm1, 0), xqs(xm1, 0), xn)
    net.arrived("xqv0", xqs(xp1, 0), xn)
    net.arrived("xqv1", xqs(xp1, 1), xn)
    net.start("xqf1", xqs(xp1, 1), xqs(xp1, 1), xv)
    net.arrived("xqn1", xqs(xm1, 1), xv)
    net.arrived("xqf0", xqs(xp2, 0), xv)
    net.arrived("xqf1", xqs(xp2, 1), xn)
    net.start("xqm", xq.at[:, core], xq.at[:, core], mate)

    def rows(xx, o):
        return pl.ds(pl.multiple_of((xx * 2 + at_y(o)) * 112, 16), 112)

    def xpa(dyl, dz):
        g_from = ((1 - yl) if dyl else yl) * 8 + (z + dz + 8) % 8
        return xp.at[core, g_from]

    net.arrived("xqm", xq.at[:, 1 - core], mate)
    for k in range(2):
        for r in range(1, 16):
            net.arrived(("t", k, r), tall.at[k, (g - r + 16) % 16], peer(16 - r))
        t = jnp.concatenate([tall[k, j].astype(F32)[:56] for j in range(16)], axis=0)
        rt = lax.dot_general(
            t.astype(BF16), xq[...].reshape(512, 896), (((0,), (1,)), ((), ())),
            preferred_element_type=F32,
        )
        right[k, rows(x, 0)] = jnp.concatenate([rt[:56], rt[64:120]], axis=0).astype(BF16)
        own = right.at[k, rows(x, 0)]
        net.start(("ry", k), own, own, yp)
        net.start(("rn", k, 0), own, own, xn)
        net.start(("rv", k, 0), own, own, xv)
        if k == 0:
            net.arrived("xpy", xpa(1, 0), yn)
            net.start(("xpn", 1, 1), xpa(1, 0), xpa(1, 0), zn)
            net.start(("xpv", 1, 1), xpa(1, 0), xpa(1, 0), zv)

    def xp_step(s):
        for dyl in range(2):
            net.arrived(("xpn", dyl, s), xpa(dyl, -s), zv)
            if s < 4:
                net.start(("xpn", dyl, s + 1), xpa(dyl, -s), xpa(dyl, -s), zn)
            if s < 4:
                net.arrived(("xpv", dyl, s), xpa(dyl, s), zn)
                if s < 3:
                    net.start(("xpv", dyl, s + 1), xpa(dyl, s), xpa(dyl, s), zv)

    def r_y(k):
        part = right.at[k, rows(x, 1)]
        net.arrived(("ry", k), part, yp)
        net.start(("rn", k, 1), part, part, xn)
        net.start(("rv", k, 1), part, part, xv)

    def r_forward(k, o):
        net.arrived(("rn", k, o), right.at[k, rows(xm1, o)], xv)
        part = right.at[k, rows(xm1, o), pl.ds(0, 256)]
        net.start(("rfn", k, o), part, part, xn)
        net.arrived(("rv", k, o), right.at[k, rows(xp1, o)], xn)
        part = right.at[k, rows(xp1, o), pl.ds(256, 256)]
        net.start(("rfv", k, o), part, part, xv)

    def r_last(k):
        for o in range(2):
            net.arrived(("rfn", k, o), right.at[k, rows(xp2, o), pl.ds(0, 256)], xv)
            net.arrived(("rfv", k, o), right.at[k, rows(xp2, o), pl.ds(256, 256)], xn)

    def compute(k):
        def tile(t, carry):
            c, h = t // 2, t % 2
            p = jnp.dot(
                xp[c, pl.ds(8 * h, 8)].reshape(256, 896), right[k], preferred_element_type=F32
            )
            zt = zb[c, pl.ds(pl.multiple_of(256 * h, 256), 256), :]
            w[pl.ds(pl.multiple_of(256 * t, 256), 256), :] = (zt * p).astype(BF16)
            return carry

        lax.fori_loop(0, 4, tile, 0)

        def mix(t, carry):
            a = pl.ds(pl.multiple_of(128 * t, 128), 128)
            mp[k, a, :] = jnp.dot(xpt[a, :], w[...], preferred_element_type=F32)
            return carry

        lax.fori_loop(0, 7, mix, 0)

    def e_one(k):
        for o in (1, 0):
            v = mp[k, rows(xp2, o), :]
            e1s[k, o, 0] = v[:, :256].astype(BF16)
            e1s[k, o, 1] = v[:, 256:].astype(BF16)
            net.start(("e1n", k, o), e1s.at[k, o, 0], e1r.at[k, o, 0], xn)
            net.start(("e1v", k, o), e1s.at[k, o, 1], e1r.at[k, o, 1], xv)

    def e_two(k):
        for o in (1, 0):
            net.arrived(("e1n", k, o), e1r.at[k, o, 0], xv)
            v = mp[k, rows(xp1, o), :]
            e2s[k, o, 0] = jnp.concatenate(
                [v[:, :256] + e1r[k, o, 0].astype(F32), v[:, 256:]], axis=1
            ).astype(BF16)
            net.start(("e2n", k, o), e2s.at[k, o, 0], e2r.at[k, o, 0], xn)
            net.arrived(("e1v", k, o), e1r.at[k, o, 1], xn)
            v = mp[k, rows(xm1, o), :]
            e2s[k, o, 1] = jnp.concatenate(
                [v[:, :256], v[:, 256:] + e1r[k, o, 1].astype(F32)], axis=1
            ).astype(BF16)
            net.start(("e2v", k, o), e2s.at[k, o, 1], e2r.at[k, o, 1], xv)

    def e_three(k):
        for o in (1, 0):
            net.arrived(("e2n", k, o), e2r.at[k, o, 0], xv)
            net.arrived(("e2v", k, o), e2r.at[k, o, 1], xn)
            v = mp[k, rows(x, o), :] + e2r[k, o, 0].astype(F32) + e2r[k, o, 1].astype(F32)
            if o == 1:
                eys[k] = v.astype(BF16)
                net.start(("ey", k), eys.at[k], eyr.at[k], yp)
            else:
                mp[k, rows(x, 0), :] = v

    def ladder(k):
        net.arrived(("ey", k), eyr.at[k], yp)
        v = mp[k, rows(x, 0), :] + eyr[k].astype(F32)
        gap = jnp.zeros((8, 512), F32)
        v = jnp.concatenate([v[:56], gap, v[56:], gap], axis=0).astype(BF16)
        lad[...] = lax.dot_general(
            xqt[...], v, (((1,), (1,)), ((), ())), preferred_element_type=F32
        )
        gap = jnp.zeros((8, 128), F32)
        for j in range(16):
            fs[k, j] = jnp.concatenate([lad[56 * j : 56 * j + 56, :], gap], axis=0).astype(BF16)
        for r in range(1, 16):
            net.start(("f", k, r), fs.at[k, (g + r) % 16], fr.at[k, r], peer(r))
        fins[k, pl.ds(0, 56), :] = lad[pl.ds(pl.multiple_of(g * 56, 8), 56), :]
        fins[k, pl.ds(56, 8), :] = gap

    xp_step(1)
    r_y(0)
    r_forward(0, 0)
    xp_step(2)
    r_y(1)
    r_forward(0, 1)
    xqt[...] = jnp.transpose(xq[...].reshape(512, 896))
    xp_step(3)
    r_forward(1, 0)
    xp_step(4)
    net.start("xpm", xp.at[core], xp.at[core], mate)
    r_forward(1, 1)
    zcopy.wait()
    net.arrived("zsw", zb.at[1 - core], mate)
    net.arrived("xpm", xp.at[1 - core], mate)
    for t in range(4):
        xpt[:, 256 * t : 256 * t + 256] = jnp.transpose(
            xp[t // 2, pl.ds(8 * (t % 2), 8)].reshape(256, 896)
        )
    r_last(0)
    compute(0)
    e_one(0)
    r_last(1)
    compute(1)
    e_one(1)
    e_two(0)
    e_two(1)
    e_three(0)
    e_three(1)
    ladder(0)
    ladder(1)
    for k in range(2):
        total = fins[k]
        for r in range(1, 16):
            net.arrived(("f", k, r), fr.at[k, r], peer(16 - r))
            total = total + fr[k, r].astype(F32)
        fins[k] = total
        net.start(("fin", k), fins.at[k], finr.at[k], mate)
    for k in range(2):
        out_ref[2 * core + k] = fins[k]
    for k in range(2):
        net.arrived(("fin", k), finr.at[k], mate)
        out_ref[2 * (1 - core) + k] = finr[k]
    net.close()


def local(amplitudes, grid_factor, metric, virt_energy, pair_energy):
    core = lax.axis_index("blk") % 2
    t = jnp.pad(jnp.transpose(amplitudes, (1, 2, 0)), ((0, 0), (0, 8), (0, 8)))
    tt = jnp.concatenate(
        [jnp.where(core == 0, t, jnp.zeros_like(t)), jnp.where(core == 1, t, jnp.zeros_like(t))],
        axis=2,
    )
    vm = pl.BlockSpec(memory_space=pltpu.VMEM)
    out = pl.pallas_call(
        kernel,
        out_shape=jax.ShapeDtypeStruct((4, 64, 128), F32),
        in_specs=[vm, vm, pl.BlockSpec(memory_space=pl.ANY)],
        out_specs=vm,
        scratch_shapes=[
            pltpu.VMEM((2, 64, 128), BF16),
            pltpu.VMEM((2, 64, 128), BF16),
            pltpu.VMEM((2, 16, 64, 128), BF16),
            pltpu.VMEM((8, 2, 32, 896), BF16),
            pltpu.VMEM((896, 512), BF16),
            pltpu.VMEM((2, 16, 32, 896), BF16),
            pltpu.VMEM((896, 1024), BF16),
            pltpu.VMEM((2, 512, 512), F32),
            pltpu.VMEM((2, 896, 512), BF16),
            pltpu.VMEM((1024, 512), BF16),
            pltpu.VMEM((2, 896, 512), F32),
            pltpu.VMEM((2, 2, 2, 112, 256), BF16),
            pltpu.VMEM((2, 2, 2, 112, 256), BF16),
            pltpu.VMEM((2, 2, 2, 112, 512), BF16),
            pltpu.VMEM((2, 2, 2, 112, 512), BF16),
            pltpu.VMEM((2, 112, 512), BF16),
            pltpu.VMEM((2, 112, 512), BF16),
            pltpu.VMEM((896, 128), F32),
            pltpu.VMEM((2, 16, 64, 128), BF16),
            pltpu.VMEM((2, 16, 64, 128), BF16),
            pltpu.VMEM((2, 64, 128), F32),
            pltpu.VMEM((2, 64, 128), F32),
            pltpu.SemaphoreType.DMA((SEMS,)),
            pltpu.SemaphoreType.DMA((SEMS,)),
            pltpu.SemaphoreType.DMA,
        ],
        compiler_params=pltpu.CompilerParams(
            collective_id=0, has_side_effects=True, vmem_limit_bytes=48 * 1024 * 1024
        ),
    )(tt, grid_factor, metric)
    ladder = jnp.where(core == 0, out[:, :56, :56], out[:, :56, 64:120])
    ladder = jnp.transpose(ladder, (2, 0, 1))
    rows, cols = amplitudes.shape[0], amplitudes.shape[2]
    first = lax.dynamic_slice_in_dim(virt_energy, lax.axis_index("blk") * rows, rows)
    second = lax.dynamic_slice_in_dim(virt_energy, lax.axis_index("grp") * cols, cols)
    denominator = first[:, None, None] + second[None, None, :] - pair_energy[None, :, None]
    return denominator * amplitudes.astype(F32) + ladder


def solution(mesh):
    in_specs = (P("blk", None, "grp"), P(("blk", "grp"), None), P("blk", "grp", None), P(), P())
    return jax.shard_map(
        local, mesh=mesh, in_specs=in_specs, out_specs=P("blk", None, "grp"), check_vma=False
    )
```

time: 240 us -> 87.8 us (0.37)
  waiting for transfers between devices: 138 us -> 0 us
  Pallas kernels: 0 us -> 83.6 us
  local copies, waits for them, and re-layouts: 30.5 us -> 3.63 us
  blocking collectives: 24 us -> 0 us
  starting transfers between devices: 23.7 us -> 0 us
  between operations: 13.2 us -> 0.06 us
  matrix products: 9.37 us -> 0 us
    pallas_call x0 -> x1, Pallas kernels: none -> 83.6 us  [local(): pl.pallas_call(kernel, out_shape=jax.ShapeDtypeStruct((4, 64, 128), F32),...]
    reduce_scatter x2 -> x0, waiting for transfers between devices: 69.7 us -> none  [own_block(): pieces = lax.psum_scatter(pieces, axes[k], scatter_dimension=0, tiled=True)]
    all_gather x1 -> x0, waiting for transfers between devices: 40.1 us -> none  [stacked_from(): pieces = lax.all_gather(pieces, axes[k], axis=0, tiled=True)]
    all_to_all x3 -> x0, waiting for transfers between devices: 28.4 us -> none  [the longest x2 19.1 us: from_everyone(): lax.all_to_all(jnp.broadcast_to(x[None], (count, *x.shape)), axis, 0, 0,...]
    all_to_all x3 -> x0, starting transfers between devices: 23.5 us -> none  [the longest x2 16.3 us: from_everyone(): lax.all_to_all(jnp.broadcast_to(x[None], (count, *x.shape)), axis, 0, 0,...]
    all_to_all x1 -> x0, blocking collectives: 18.4 us -> none  [from_everyone(): lax.all_to_all(jnp.broadcast_to(x[None], (count, *x.shape)), axis, 0, 0,...]
    dot_general x3 -> x0, matrix products: 9.37 us -> none  [the longest x1 7.54 us: local(): jnp.einsum('kpq,qb->bkp', weighted, columns, preferred_element_type=jnp.f...]
    transpose x3 -> x0, local copies, waits for them, and re-layouts: 8.66 us -> none  [the longest x1 4.3 us: own_block(): pieces = pieces.transpose(*sequence, *range(len(axes), pieces.ndim))]
  transfers between devices with their start and end apart: 6 -> 0, of which waited for: 5 -> 0; matrix products, arithmetic and copies ran while one was open for 4% -> 0% of each run, Pallas kernels for 0% -> 0%
where the time goes in v1:
time: 87.8 us; the launch traced here: 87.6 us
  Pallas kernels  83.6 us (95%)
  local copies, waits for them, and re-layouts  3.63 us (4%)
    pallas_call x1, Pallas kernels, local(): pl.pallas_call(kernel, out_shape=jax.ShapeDtypeStruct((4, 64, 128), F32),...  83.6 us
    unnamed x9, local copies, waits for them, and re-layouts  2.06 us

profile of v1, /device:TPU:1, one launch (start us, length us, event | category | flops | bytes accessed | tf_op | source)
XLA Modules:
  0.0 87.6 jit_solution(11777015431601564596)
XLA Ops:
  0.0 0.0 copy-start.2
  0.0 0.8 fusion
  0.8 0.1 broadcast_add_fusion
  0.9 0.0 copy-done.2
  0.9 0.1 copy.6
  1.1 0.0 copy-start.1
  1.1 0.1 pad_maximum_fusion.tt_ref
  1.2 0.7 copy-done.1
  1.9 0.0 copy-start
  1.9 1.2 %copy-done = f32[512,1,512]{2,1,0:T(1,128)S(1)} copy-done((f32[512,1,512]{2,1,0:T(1,128)S(1)}, f32[512,1,512]{2,1,0:T(1,128)}, u32[]{:S(2)}) %copy-start) | copy-done | bytes 1048600
  3.1 0.0 copy-start.3
  3.1 83.6 %shard_map.55 = f32[4,64,128]{2,1,0:T(8,128)S(1)} custom-call(bf16[4,64,128]{2,1,0:T(8,128)(2,1)S(1)} %pad_maximum_fusion.tt_ref, bf16[32,896]{1,0:T(8,128)(2,1)S(1)} %copy-done.1, f32[512,1,512]{2,1,0:T(1,128)S(1)} %copy-done), custom_call_target="tpu_custom_call" | custom-call | tf_op jit(solution)/shard_map/pallas_call | solution.py:296
  86.8 0.0 copy-done.3
  86.8 0.1 bitcast_add_fusion
  86.9 0.7 copy.8
  (1 shorter events, 0.0 us)
Async XLA Ops:
  0.0 0.9 %copy-start.2 = (bf16[56,4,56]{2,1,0:T(4,128)(2,1)S(1)}, bf16[56,4,56]{2,1,0:T(4,128)(2,1)}, u32[]{:S(2)}) copy-start(bf16[56,4,56]{2,1,0:T(4,128)(2,1)} %param.5) | copy-start | bytes 75268
  1.1 0.8 copy-start.1
  1.9 1.2 %copy-start = (f32[512,1,512]{2,1,0:T(1,128)S(1)}, f32[512,1,512]{2,1,0:T(1,128)}, u32[]{:S(2)}) copy-start(f32[512,1,512]{2,1,0:T(1,128)} %z_hbm.1) | copy-start | bytes 3145732
  3.1 83.6 %copy-start.3 = (f32[4]{0:T(128)S(1)}, f32[4]{0:T(128)}, u32[]{:S(2)}) copy-start(f32[4]{0:T(128)} %param.9) | copy-start | bytes 52

commit v2 on v0

v2 whole, which is shorter than its diff:
```python
import functools

import jax
import jax.numpy as jnp
from jax import lax
from jax.experimental import pallas as pl
from jax.experimental.pallas import tpu as pltpu
from jax.sharding import PartitionSpec as P

MESH = pl.DeviceIdType.MESH
F32 = jnp.float32
BF16 = jnp.bfloat16
SEMS = 200


class Links:
    def __init__(self, send, recv):
        self.send, self.recv, self.ids, self.open = send, recv, {}, []

    def index(self, key):
        assert len(self.ids) < SEMS
        return self.ids.setdefault(key, len(self.ids))

    def copy(self, key, src, dst, dev):
        i = self.index(key)
        return pltpu.make_async_remote_copy(
            src_ref=src, dst_ref=dst, send_sem=self.send.at[i], recv_sem=self.recv.at[i],
            device_id=dev, device_id_type=MESH,
        )

    def start(self, key, src, dst, dev):
        c = self.copy(key, src, dst, dev)
        c.start()
        self.open.append(c)

    def arrived(self, key, dst, dev):
        self.copy(key, dst, dst, dev).wait_recv()

    def close(self):
        for c in self.open:
            c.wait_send()


def kernel(
    tt_ref, x_ref, z_hbm, out_ref,
    tall, xq, xqt, xp, xpt, zb, right, w, mp,
    e1s, e1r, e2s, e2r, e3s, e3r, eys, eyr, lad, fs, fy, fr, fins, finr,
    send, recv, zsem,
):
    b, g = lax.axis_index("blk"), lax.axis_index("grp")
    core, yh, x = b % 2, (b // 2) % 2, b // 4
    yl, z = g // 8, g % 8
    m = x * 2 + yh
    net = Links(send, recv)

    def at(dx, dy, dc=0):
        yy = 1 - yh if dy else yh
        cc = 1 - core if dc else core
        return {"blk": ((x + dx + 4) % 4) * 4 + yy * 2 + cc, "grp": g}

    def up(dz, dyl=0, dc=0):
        return {
            "blk": b + 1 - 2 * core if dc else b,
            "grp": ((1 - yl) if dyl else yl) * 8 + (z + dz) % 8,
        }

    mate, yp = at(0, 0, 1), at(0, 1)
    zn, zv, yn = up(1), up(7), up(0, 1)
    around = [(2, 1), (3, 1), (1, 1), (2, 0), (3, 0), (1, 0)]

    def rows(dx, o, first=0, count=112):
        yy = 1 - yh if o else yh
        return pl.ds(pl.multiple_of((((x + dx + 4) % 4) * 2 + yy) * 112 + first, 16), count)

    def xqa(dx, dy):
        return xq.at[((x + dx + 4) % 4) * 2 + ((1 - yh) if dy else yh), core]

    def gi(dz, dyl):
        return ((1 - yl) if dyl else yl) * 8 + (z + dz + 8) % 8

    def xpa(dyl, dz):
        return xp.at[core, gi(dz, dyl)]

    zcopy = pltpu.make_async_copy(z_hbm.at[:, 0, :], zb.at[core], zsem)
    zcopy.start()

    barrier = pltpu.get_barrier_semaphore()
    near = [mate, yn] + [at(dx, 0) for dx in range(1, 4)]
    near += [yp] + [up(dz, 0, dc) for dz in range(1, 8) for dc in range(2)]
    with jax.named_scope("barrier"):
        for dev in near:
            pl.semaphore_signal(barrier, inc=1, device_id=dev, device_id_type=MESH)
        pl.semaphore_wait(barrier, len(near))

    far = (4, 3, 5, 2, 6, 1, 7)

    def t_send(k):
        net.start(("t", k, 0, 1), tt_ref.at[2 * (1 - core) + k], tall.at[k, core, g], mate)
        for dz in far:
            for dc in range(2):
                pair = 2 * ((1 - core) if dc else core) + k
                net.start(("t", k, dz, dc), tt_ref.at[pair], tall.at[k, core, g], up(dz, 0, dc))
        tall[k, core, g] = tt_ref[2 * core + k]

    def t_forward(k, dz):
        j = gi(-dz, 0)
        for dc in range(2):
            if dz or dc:
                part = tall.at[k, (1 - core) if dc else core, j]
                net.arrived(("t", k, dz, dc), part, up(8 - dz, 0, dc))
        net.start(("ty", k, dz), tall.at[k, :, j], tall.at[k, :, j], yn)

    t_send(0)
    net.start("xpy", x_ref, xpa(0, 0), yn)
    for dx, dy in ((0, 1), (1, 0), (3, 0), (2, 0)):
        net.start(("xq", dx, dy), x_ref, xqa(0, 0), at(dx, dy))
    net.start(("xqm", 0, 0), x_ref, xqa(0, 0), mate)
    net.start(("xpn", 0, 1), x_ref, xpa(0, 0), zn)
    net.start(("xpv", 0, 1), x_ref, xpa(0, 0), zv)
    net.start(("xpm", 0, 0), x_ref, xpa(0, 0), mate)
    xq[m, core] = x_ref[...]
    xp[core, g] = x_ref[...]

    def xq_forward(dx, dy):
        part = xqa(-dx, dy)
        net.arrived(("xq", dx, dy), part, at(4 - dx, 0 if dx else dy))
        if (dx, dy) == (0, 1):
            for to in (1, 3, 2):
                net.start(("xq", to, 1), part, part, at(to, 0))
        net.start(("xqm", dx, dy), part, part, mate)

    lane = lax.broadcasted_iota(jnp.int32, (512, 128), 1)

    def first(k):
        for dz in (0,) + far:
            net.arrived(("ty", k, dz), tall.at[k, :, gi(-dz, 1)], yn)
        one = tall[k, 0].reshape(512, 128).astype(F32)
        two = tall[k, 1].reshape(512, 128).astype(F32)
        top = jnp.where(lane < 64, one, pltpu.roll(two, 64, 1))
        low = jnp.where(lane < 64, pltpu.roll(one, 64, 1), two)
        t = jnp.concatenate(
            [v for j in range(16) for v in (top[32 * j : 32 * j + 32], low[32 * j : 32 * j + 24])],
            axis=0,
        )
        rt = lax.dot_general(
            t.astype(BF16), xq[...].reshape(512, 896), (((0,), (1,)), ((), ())),
            preferred_element_type=F32,
        )
        right[k, rows(0, 0)] = jnp.concatenate([rt[:56], rt[64:120]], axis=0).astype(BF16)
        own = right.at[k, rows(0, 0)]
        net.start(("ry", k, 0), own, own, yp)
        for dx in (1, 3, 2):
            net.start(("rx", k, dx), own, own, at(dx, 0))

    def xp_mate(dyl, dz):
        net.start(("xpm", dyl, dz), xpa(dyl, dz), xpa(dyl, dz), mate)

    def xp_y():
        part = xpa(1, 0)
        net.arrived("xpy", part, yn)
        net.start(("xpn", 1, 1), part, part, zn)
        net.start(("xpv", 1, 1), part, part, zv)
        xp_mate(1, 0)

    def xp_step(s, dyl):
        if s < 4 or dyl == 0:
            part = xpa(dyl, -s)
            net.arrived(("xpn", dyl, s), part, zv)
            if s < 3 or (s == 3 and dyl == 0):
                net.start(("xpn", dyl, s + 1), part, part, zn)
            xp_mate(dyl, -s)
        if s < 4 or dyl == 1:
            part = xpa(dyl, s)
            net.arrived(("xpv", dyl, s), part, zn)
            if s < 3 or (s == 3 and dyl == 1):
                net.start(("xpv", dyl, s + 1), part, part, zv)
            xp_mate(dyl, s)

    def r_y(k):
        net.arrived(("ry", k, 0), right.at[k, rows(0, 1)], yp)
        part = right.at[k, rows(0, 1, 0, 48)]
        for dx in (1, 3, 2):
            net.start(("rz", k, dx), part, part, at(dx, 0))

    def r_x(k, *ways):
        for dx in ways:
            net.arrived(("rx", k, dx), right.at[k, rows(-dx, 0)], at(4 - dx, 0))
            part = right.at[k, rows(-dx, 0, 48, 64)]
            net.start(("ry", k, dx), part, part, yp)

    def r_last(k):
        for dx in (1, 3, 2):
            net.arrived(("rz", k, dx), right.at[k, rows(-dx, 1, 0, 48)], at(4 - dx, 0))
        for dx in (1, 3, 2):
            net.arrived(("ry", k, dx), right.at[k, rows(-dx, 1, 48, 64)], yp)

    def weigh(k, c):
        p = jnp.dot(xp[c].reshape(512, 896), right[k], preferred_element_type=F32)
        w[512 * c : 512 * c + 512, :] = (zb[c] * p).astype(BF16)

    def mix(k, t):
        a = pl.ds(448 * t, 448)
        mp[k, a, :] = jnp.dot(xpt[a, :], w[...], preferred_element_type=F32)

    order = (2, 1, 3, 0)

    def e_start(k):
        for i, dx in enumerate(order):
            eys[k, i] = mp[k, rows(dx, 1, 48, 64), :].astype(BF16)
            net.start(("ey", k, dx), eys.at[k, i], eyr.at[k, i], yp)
            if dx:
                for o in range(2):
                    e1s[k, i, o] = mp[k, rows(dx, o, 0, 48), :].astype(BF16)
                net.start(("e1", k, dx), e1s.at[k, i], e1r.at[k, i], at(dx, 0))

    def e_y(k, dx):
        i = order.index(dx)
        net.arrived(("ey", k, dx), eyr.at[k, i], yp)
        return mp[k, rows(dx, 0, 48, 64), :] + eyr[k, i].astype(F32)

    def e_two(k):
        for i, dx in enumerate(order[:3]):
            e2s[k, i] = e_y(k, dx).astype(BF16)
            net.start(("e2", k, dx), e2s.at[k, i], e2r.at[k, i], at(dx, 0))

    def e_three(k):
        v = mp[k, rows(0, 1, 0, 48), :]
        for i, dx in enumerate(order[:3]):
            net.arrived(("e1", k, dx), e1r.at[k, i], at(4 - dx, 0))
            v = v + e1r[k, i, 1].astype(F32)
        e3s[k] = v.astype(BF16)
        net.start(("e3", k), e3s.at[k], e3r.at[k], yp)

    def e_last(k):
        v = e_y(k, 0)
        for i, dx in enumerate(order[:3]):
            net.arrived(("e2", k, dx), e2r.at[k, i], at(4 - dx, 0))
            v = v + e2r[k, i].astype(F32)
        u = mp[k, rows(0, 0, 0, 48), :]
        for i in range(3):
            u = u + e1r[k, i, 0].astype(F32)
        net.arrived(("e3", k), e3r.at[k], yp)
        return jnp.concatenate([u + e3r[k].astype(F32), v], axis=0)

    def ladder(k, v):
        gap = jnp.zeros((8, 512), F32)
        v = jnp.concatenate([v[:56], gap, v[56:], gap], axis=0).astype(BF16)
        lad[k] = lax.dot_general(
            xqt[...], v, (((1,), (1,)), ((), ())), preferred_element_type=F32
        )
        gap = jnp.zeros((8, 128), F32)
        for dz in range(8):
            j = gi(dz, 1)
            v = lad[k, pl.ds(pl.multiple_of(j * 56, 8), 56), :]
            fs[k, j] = jnp.concatenate([v, gap], axis=0).astype(BF16)
        for dz in far + (0,):
            net.start(("fy", k, dz), fs.at[k, gi(dz, 1)], fy.at[k, dz], yn)

    def fold(k):
        for dz in far + (0,):
            j = gi(dz, 0)
            net.arrived(("fy", k, dz), fy.at[k, dz], yn)
            v = lad[k, pl.ds(pl.multiple_of(j * 56, 8), 56), :] + fy[k, dz, 0:56].astype(F32)
            v = jnp.concatenate([v, jnp.zeros((8, 128), F32)], axis=0)
            if dz:
                fs[k, j] = v.astype(BF16)
                net.start(("f", k, dz), fs.at[k, j], fr.at[k, dz], up(dz))
            else:
                fins[k] = v

    def scoped(name, f, *args):
        with jax.named_scope(name):
            return f(*args)

    scoped("xp_y", xp_y)
    scoped("xq_y", xq_forward, 0, 1)
    with jax.named_scope("t0_xq"):
        t_forward(0, 0)
        for i, dz in enumerate(far[::-1]):
            t_forward(0, dz)
            if i < 3:
                xq_forward(*around[::-1][i])
    scoped("xp_step10", xp_step, 1, 0)
    scoped("xp_step11", xp_step, 1, 1)
    t_send(1)
    with jax.named_scope("xq_far"):
        for dx, dy in around[2::-1]:
            xq_forward(dx, dy)
    with jax.named_scope("xqm_wait"):
        for dx, dy in around + [(0, 1), (0, 0)]:
            part = xq.at[((x - dx + 4) % 4) * 2 + ((1 - yh) if dy else yh), 1 - core]
            net.arrived(("xqm", dx, dy), part, mate)
    scoped("first0", first, 0)
    scoped("xp_step20", xp_step, 2, 0)
    scoped("xp_step21", xp_step, 2, 1)
    with jax.named_scope("xqt"):
        xqt[...] = jnp.transpose(xq[...].reshape(512, 896))
    net.start("zsw", z_hbm.at[:, 0, :], zb.at[core], mate)
    with jax.named_scope("t1"):
        for dz in (0,) + far[::-1]:
            t_forward(1, dz)
    scoped("r_x01", r_x, 0, 1)
    scoped("xp_step30", xp_step, 3, 0)
    scoped("r_x03", r_x, 0, 3)
    scoped("xp_step31", xp_step, 3, 1)
    scoped("r_y0", r_y, 0)
    scoped("r_x02", r_x, 0, 2)
    scoped("first1", first, 1)
    scoped("xp_step40", xp_step, 4, 0)
    scoped("xp_step41", xp_step, 4, 1)
    with jax.named_scope("z_wait"):
        zcopy.wait()
        net.arrived("zsw", zb.at[1 - core], mate)
    scoped("r_x11", r_x, 1, 1)
    with jax.named_scope("xpm_wait"):
        for s in range(-4, 5):
            for dyl in range(2):
                if (s, dyl) not in ((4, 0), (-4, 1)):
                    net.arrived(("xpm", dyl, s), xp.at[1 - core, gi(s, dyl)], mate)
    with jax.named_scope("xpt"):
        for t in range(4):
            xpt[:, 256 * t : 256 * t + 256] = jnp.transpose(
                xp[t // 2, pl.ds(8 * (t % 2), 8)].reshape(256, 896)
            )
    scoped("r_x13", r_x, 1, 3)
    scoped("r_last0", r_last, 0)
    scoped("weigh00", weigh, 0, 0)
    scoped("r_y1", r_y, 1)
    scoped("weigh01", weigh, 0, 1)
    scoped("r_x12", r_x, 1, 2)
    scoped("mix00", mix, 0, 0)
    scoped("mix01", mix, 0, 1)
    scoped("e_start0", e_start, 0)
    scoped("r_last1", r_last, 1)
    scoped("weigh10", weigh, 1, 0)
    scoped("weigh11", weigh, 1, 1)
    scoped("mix10", mix, 1, 0)
    scoped("mix11", mix, 1, 1)
    scoped("e_start1", e_start, 1)
    scoped("e_two0", e_two, 0)
    scoped("e_three0", e_three, 0)
    scoped("e_two1", e_two, 1)
    scoped("e_three1", e_three, 1)
    v0 = scoped("e_last0", e_last, 0)
    scoped("ladder0", ladder, 0, v0)
    v1 = scoped("e_last1", e_last, 1)
    scoped("ladder1", ladder, 1, v1)
    scoped("fold0", fold, 0)
    scoped("fold1", fold, 1)
    for k in range(2):
        total = fins[k]
        with jax.named_scope(f"f_wait{k}"):
            for dz in far:
                net.arrived(("f", k, dz), fr.at[k, dz], up(8 - dz))
                total = total + fr[k, dz].astype(F32)
        fins[k] = total
        net.start(("fin", k), fins.at[k], finr.at[k], mate)
    for k in range(2):
        out_ref[2 * core + k] = fins[k]
    with jax.named_scope("fin"):
        for k in range(2):
            net.arrived(("fin", k), finr.at[k], mate)
            out_ref[2 * (1 - core) + k] = finr[k]
    with jax.named_scope("close"):
        net.close()


def local(amplitudes, grid_factor, metric, virt_energy, pair_energy):
    core = lax.axis_index("blk") % 2
    t = jnp.pad(jnp.transpose(amplitudes, (1, 2, 0)), ((0, 0), (0, 8), (0, 8)))
    tt = jnp.concatenate([t[:, :32], t[:, 32:]], axis=2)
    vm = pl.BlockSpec(memory_space=pltpu.VMEM)
    out = pl.pallas_call(
        kernel,
        out_shape=jax.ShapeDtypeStruct((4, 64, 128), F32),
        in_specs=[vm, vm, pl.BlockSpec(memory_space=pltpu.HBM)],
        out_specs=vm,
        scratch_shapes=[
            pltpu.VMEM((2, 2, 16, 32, 128), BF16),
            pltpu.VMEM((8, 2, 32, 896), BF16),
            pltpu.VMEM((896, 512), BF16),
            pltpu.VMEM((2, 16, 32, 896), BF16),
            pltpu.VMEM((896, 1024), BF16),
            pltpu.VMEM((2, 512, 512), F32),
            pltpu.VMEM((2, 896, 512), BF16),
            pltpu.VMEM((1024, 512), BF16),
            pltpu.VMEM((2, 896, 512), F32),
            pltpu.VMEM((2, 3, 2, 48, 512), BF16),
            pltpu.VMEM((2, 3, 2, 48, 512), BF16),
            pltpu.VMEM((2, 3, 64, 512), BF16),
            pltpu.VMEM((2, 3, 64, 512), BF16),
            pltpu.VMEM((2, 48, 512), BF16),
            pltpu.VMEM((2, 48, 512), BF16),
            pltpu.VMEM((2, 4, 64, 512), BF16),
            pltpu.VMEM((2, 4, 64, 512), BF16),
            pltpu.VMEM((2, 896, 128), F32),
            pltpu.VMEM((2, 16, 64, 128), BF16),
            pltpu.VMEM((2, 8, 64, 128), BF16),
            pltpu.VMEM((2, 8, 64, 128), BF16),
            pltpu.VMEM((2, 64, 128), F32),
            pltpu.VMEM((2, 64, 128), F32),
            pltpu.SemaphoreType.DMA((SEMS,)),
            pltpu.SemaphoreType.DMA((SEMS,)),
            pltpu.SemaphoreType.DMA,
        ],
        compiler_params=pltpu.CompilerParams(
            collective_id=0, has_side_effects=True, vmem_limit_bytes=65000 * 1024
        ),
    )(tt, grid_factor, metric)
    ladder = jnp.where(core == 0, out[:, :56, :56], out[:, :56, 64:120])
    ladder = jnp.transpose(ladder, (2, 0, 1))
    rows, cols = amplitudes.shape[0], amplitudes.shape[2]
    first = lax.dynamic_slice_in_dim(virt_energy, lax.axis_index("blk") * rows, rows)
    second = lax.dynamic_slice_in_dim(virt_energy, lax.axis_index("grp") * cols, cols)
    denominator = first[:, None, None] + second[None, None, :] - pair_energy[None, :, None]
    return denominator * amplitudes.astype(F32) + ladder


def solution(mesh):
    in_specs = (P("blk", None, "grp"), P(("blk", "grp"), None), P("blk", "grp", None), P(), P())
    return jax.shard_map(
        local, mesh=mesh, in_specs=in_specs, out_specs=P("blk", None, "grp"), check_vma=False
    )
```

time: 240 us -> 76.2 us (0.32)
  waiting for transfers between devices: 138 us -> 0 us
  Pallas kernels: 0 us -> 72.4 us
  local copies, waits for them, and re-layouts: 30.5 us -> 1.71 us
  blocking collectives: 24 us -> 0 us
  starting transfers between devices: 23.7 us -> 0 us
  between operations: 13.2 us -> 0.04 us
  matrix products: 9.37 us -> 0 us
    pallas_call x0 -> x1, Pallas kernels: none -> 72.4 us  [local(): pl.pallas_call(kernel, out_shape=jax.ShapeDtypeStruct((4, 64, 128), F32),...]
    reduce_scatter x2 -> x0, waiting for transfers between devices: 69.7 us -> none  [own_block(): pieces = lax.psum_scatter(pieces, axes[k], scatter_dimension=0, tiled=True)]
    all_gather x1 -> x0, waiting for transfers between devices: 40.1 us -> none  [stacked_from(): pieces = lax.all_gather(pieces, axes[k], axis=0, tiled=True)]
    all_to_all x3 -> x0, waiting for transfers between devices: 28.4 us -> none  [the longest x2 19.1 us: from_everyone(): lax.all_to_all(jnp.broadcast_to(x[None], (count, *x.shape)), axis, 0, 0,...]
    all_to_all x3 -> x0, starting transfers between devices: 23.5 us -> none  [the longest x2 16.3 us: from_everyone(): lax.all_to_all(jnp.broadcast_to(x[None], (count, *x.shape)), axis, 0, 0,...]
    all_to_all x1 -> x0, blocking collectives: 18.4 us -> none  [from_everyone(): lax.all_to_all(jnp.broadcast_to(x[None], (count, *x.shape)), axis, 0, 0,...]
    dot_general x3 -> x0, matrix products: 9.37 us -> none  [the longest x1 7.54 us: local(): jnp.einsum('kpq,qb->bkp', weighted, columns, preferred_element_type=jnp.f...]
    unnamed x9 -> x5, local copies, waits for them, and re-layouts: 9.32 us -> 0.12 us
  transfers between devices with their start and end apart: 6 -> 0, of which waited for: 5 -> 0; matrix products, arithmetic and copies ran while one was open for 4% -> 0% of each run, Pallas kernels for 0% -> 0%
where the time goes in v2:
time: 76.2 us; the launch traced here: 76 us
  Pallas kernels  72.4 us (95%)
  other arithmetic  1.85 us (2%)
  local copies, waits for them, and re-layouts  1.71 us (2%)
    pallas_call x1, Pallas kernels, local(): pl.pallas_call(kernel, out_shape=jax.ShapeDtypeStruct((4, 64, 128), F32),...  72.4 us

profile of v2, /device:TPU:1, one launch (start us, length us, event | category | flops | bytes accessed | tf_op | source)
XLA Modules:
  0.0 76.0 jit_solution(4751091383194127189)
XLA Ops:
  0.0 0.0 copy-start
  0.0 0.8 %fusion = (f32[56]{0:T(128)S(1)}, f32[56]{0:T(128)S(1)}) fusion(f32[896]{0:T(1024)} %param.8, s32[]{:T(128)S(6)} %select_n.21, s32[]{:T(128)S(6)} %select_n.22), kind=kLoop, calls=%fused_computation.5 | loop fusion | bytes 904 | tf_op jit(solution)/shard_map/dynamic_slice | solution.py:413
  0.8 0.1 broadcast_add_fusion
  0.9 0.0 copy-done
  0.9 0.1 copy.6
  1.1 0.7 pad_maximum_fusion.tt_ref
  1.8 0.0 copy-start.1
  1.8 72.4 %shard_map.55 = f32[4,64,128]{2,1,0:T(8,128)} custom-call(bf16[4,32,128]{2,1,0:T(8,128)(2,1)} %pad_maximum_fusion.tt_ref, bf16[32,896]{1,0:T(8,128)(2,1)} %x_ref.1, f32[512,1,512]{2,1,0:T(1,128)} %z_hbm.1), custom_call_target="tpu_custom_call" | custom-call | tf_op jit(solution)/shard_map/pallas_call | solution.py:373
  74.1 0.0 copy-done.1
  74.1 1.1 %bitcast_add_fusion = f32[56,4,56]{0,2,1:T(8,128)S(1)} fusion(f32[4,64,128]{2,1,0:T(8,128)} %shard_map.55, bf16[56,4,56]{0,2,1:T(8,128)(2,1)S(1)} %copy.6, f32[4]{0:T(128)S(1)} %copy-done.1, f32[56,56]{0,1:T(8,128)S(1)} %broadcast_add_fusion, pred[]{:T(512)S(6)} %eq.5), kind=kLoop, calls=%fused_computation | loop fusion | flops 62720 | bytes 188177 | tf_op jit(solution)/shard_map/add | solution.py:416
  75.2 0.7 copy.8
  (1 shorter events, 0.0 us)
Async XLA Ops:
  0.0 0.9 %copy-start = (bf16[56,4,56]{2,1,0:T(4,128)(2,1)S(1)}, bf16[56,4,56]{2,1,0:T(4,128)(2,1)}, u32[]{:S(2)}) copy-start(bf16[56,4,56]{2,1,0:T(4,128)(2,1)} %param.5) | copy-start | bytes 75268
  1.8 72.4 %copy-start.1 = (f32[4]{0:T(128)S(1)}, f32[4]{0:T(128)}, u32[]{:S(2)}) copy-start(f32[4]{0:T(128)} %param.9) | copy-start | bytes 52

commit v3 on v2

--- a/solution.py
+++ b/solution.py
@@ -39,13 +39,15 @@
     def close(self):
         for c in self.open:
             c.wait_send()
+        self.open = []
 
 
 def kernel(
-    tt_ref, x_ref, z_hbm, out_ref,
+    amp_hbm, x_hbm, z_hbm, ve_hbm, pe_hbm, out_ref,
+    amp, x_ref, ve, pe, tt_ref, own_amp, base,
     tall, xq, xqt, xp, xpt, zb, right, w, mp,
     e1s, e1r, e2s, e2r, e3s, e3r, eys, eyr, lad, fs, fy, fr, fins, finr,
-    send, recv, zsem,
+    send, recv, local_sem,
 ):
     b, g = lax.axis_index("blk"), lax.axis_index("grp")
     core, yh, x = b % 2, (b // 2) % 2, b // 4
@@ -81,15 +83,33 @@
     def xpa(dyl, dz):
         return xp.at[core, gi(dz, dyl)]
 
-    zcopy = pltpu.make_async_copy(z_hbm.at[:, 0, :], zb.at[core], zsem)
-    zcopy.start()
-
+    def fetch(i, src, dst):
+        c = pltpu.make_async_copy(src, dst, local_sem.at[i])
+        c.start()
+        return c
+
+    acopy, xcopy = fetch(0, amp_hbm, amp), fetch(1, x_hbm, x_ref)
     barrier = pltpu.get_barrier_semaphore()
     near = [mate, yn] + [at(dx, 0) for dx in range(1, 4)]
     near += [yp] + [up(dz, 0, dc) for dz in range(1, 8) for dc in range(2)]
     with jax.named_scope("barrier"):
         for dev in near:
             pl.semaphore_signal(barrier, inc=1, device_id=dev, device_id_type=MESH)
+        vcopy, pcopy = fetch(2, ve_hbm, ve.at[pl.ds(0, 7)]), fetch(3, pe_hbm, pe)
+        zcopy = fetch(4, z_hbm.at[:, 0, :], zb.at[core])
+        acopy.wait()
+        eye = (
+            lax.broadcasted_iota(jnp.int32, (56, 64), 0)
+            == lax.broadcasted_iota(jnp.int32, (56, 64), 1)
+        ).astype(BF16)
+        for k in range(4):
+            t = lax.dot_general(
+                amp[:, k, :], eye, (((0,), (0,)), ((), ())), preferred_element_type=F32
+            )
+            own_amp[k] = t
+            t = jnp.concatenate([t, jnp.zeros((8, 64), F32)], axis=0)
+            tt_ref[k] = jnp.concatenate([t[:32], t[32:]], axis=1).astype(BF16)
+        xcopy.wait()
         pl.semaphore_wait(barrier, len(near))
 
     far = (4, 3, 5, 2, 6, 1, 7)
@@ -295,6 +315,23 @@
     scoped("xp_step21", xp_step, 2, 1)
     with jax.named_scope("xqt"):
         xqt[...] = jnp.transpose(xq[...].reshape(512, 896))
+    with jax.named_scope("energies"):
+        vcopy.wait()
+        pcopy.wait()
+
+        def run(start):
+            r, off = start // 128, start % 128
+            lane = lax.broadcasted_iota(jnp.int32, (8, 128), 1)
+            one = jnp.broadcast_to(ve[pl.ds(r, 1), :], (8, 128))
+            two = jnp.broadcast_to(ve[pl.ds(jnp.minimum(r + 1, 6), 1), :], (8, 128))
+            shift = (128 - off) % 128
+            return jnp.where(lane < 128 - off, pltpu.roll(one, shift, 1), pltpu.roll(two, shift, 1))
+
+        first_e = run(b * 56)[0:1, :64]
+        second_e = jnp.transpose(jnp.broadcast_to(run(g * 56)[0:1], (128, 128)))[:56, :64]
+        both = second_e + first_e
+        for k in range(4):
+            base[k] = (both - pe[k]) * own_amp[k]
     net.start("zsw", z_hbm.at[:, 0, :], zb.at[core], mate)
     with jax.named_scope("t1"):
         for dz in (0,) + far[::-1]:
@@ -311,7 +348,6 @@
     with jax.named_scope("z_wait"):
         zcopy.wait()
         net.arrived("zsw", zb.at[1 - core], mate)
-    scoped("r_x11", r_x, 1, 1)
     with jax.named_scope("xpm_wait"):
         for s in range(-4, 5):
             for dyl in range(2):
@@ -322,9 +358,10 @@
             xpt[:, 256 * t : 256 * t + 256] = jnp.transpose(
                 xp[t // 2, pl.ds(8 * (t % 2), 8)].reshape(256, 896)
             )
-    scoped("r_x13", r_x, 1, 3)
     scoped("r_last0", r_last, 0)
     scoped("weigh00", weigh, 0, 0)
+    scoped("r_x11", r_x, 1, 1)
+    scoped("r_x13", r_x, 1, 3)
     scoped("r_y1", r_y, 1)
     scoped("weigh01", weigh, 0, 1)
     scoped("r_x12", r_x, 1, 2)
@@ -347,6 +384,7 @@
     scoped("ladder1", ladder, 1, v1)
     scoped("fold0", fold, 0)
     scoped("fold1", fold, 1)
+    scoped("close1", net.close)
     for k in range(2):
         total = fins[k]
         with jax.named_scope(f"f_wait{k}"):
@@ -355,27 +393,36 @@
                 total = total + fr[k, dz].astype(F32)
         fins[k] = total
         net.start(("fin", k), fins.at[k], finr.at[k], mate)
+    def finish(pair, v):
+        v = jnp.where(core == 0, v[:56, :64], v[:56, 64:]) + base[pair]
+        out_ref[pair] = v[:, :56]
+
     for k in range(2):
-        out_ref[2 * core + k] = fins[k]
+        finish(2 * core + k, fins[k])
     with jax.named_scope("fin"):
         for k in range(2):
             net.arrived(("fin", k), finr.at[k], mate)
-            out_ref[2 * (1 - core) + k] = finr[k]
+            finish(2 * (1 - core) + k, finr[k])
     with jax.named_scope("close"):
         net.close()
 
 
 def local(amplitudes, grid_factor, metric, virt_energy, pair_energy):
-    core = lax.axis_index("blk") % 2
-    t = jnp.pad(jnp.transpose(amplitudes, (1, 2, 0)), ((0, 0), (0, 8), (0, 8)))
-    tt = jnp.concatenate([t[:, :32], t[:, 32:]], axis=2)
-    vm = pl.BlockSpec(memory_space=pltpu.VMEM)
+    rows, pairs, cols = amplitudes.shape
+    hbm = pl.BlockSpec(memory_space=pltpu.HBM)
     out = pl.pallas_call(
         kernel,
-        out_shape=jax.ShapeDtypeStruct((4, 64, 128), F32),
-        in_specs=[vm, vm, pl.BlockSpec(memory_space=pltpu.HBM)],
-        out_specs=vm,
+        out_shape=jax.ShapeDtypeStruct((pairs, cols, rows), F32),
+        in_specs=[hbm] * 5,
+        out_specs=pl.BlockSpec(memory_space=pltpu.VMEM),
         scratch_shapes=[
+            pltpu.VMEM((56, 4, 56), BF16),
+            pltpu.VMEM((32, 896), BF16),
+            pltpu.VMEM((8, 128), F32),
+            pltpu.SMEM((4,), F32),
+            pltpu.VMEM((4, 32, 128), BF16),
+            pltpu.VMEM((4, 56, 64), F32),
+            pltpu.VMEM((4, 56, 64), F32),
             pltpu.VMEM((2, 2, 16, 32, 128), BF16),
             pltpu.VMEM((8, 2, 32, 896), BF16),
             pltpu.VMEM((896, 512), BF16),
@@ -401,19 +448,13 @@
             pltpu.VMEM((2, 64, 128), F32),
             pltpu.SemaphoreType.DMA((SEMS,)),
             pltpu.SemaphoreType.DMA((SEMS,)),
-            pltpu.SemaphoreType.DMA,
+            pltpu.SemaphoreType.DMA((5,)),
         ],
         compiler_params=pltpu.CompilerParams(
             collective_id=0, has_side_effects=True, vmem_limit_bytes=65000 * 1024
         ),
-    )(tt, grid_factor, metric)
-    ladder = jnp.where(core == 0, out[:, :56, :56], out[:, :56, 64:120])
-    ladder = jnp.transpose(ladder, (2, 0, 1))
-    rows, cols = amplitudes.shape[0], amplitudes.shape[2]
-    first = lax.dynamic_slice_in_dim(virt_energy, lax.axis_index("blk") * rows, rows)
-    second = lax.dynamic_slice_in_dim(virt_energy, lax.axis_index("grp") * cols, cols)
-    denominator = first[:, None, None] + second[None, None, :] - pair_energy[None, :, None]
-    return denominator * amplitudes.astype(F32) + ladder
+    )(amplitudes, grid_factor, metric, virt_energy.reshape(7, 128), pair_energy)
+    return jnp.transpose(out, (2, 0, 1))
 
 
 def solution(mesh):

time: 76.2 us -> 73.1 us (0.959)
  other arithmetic: 1.85 us -> 0 us
  Pallas kernels: 72.4 us -> 71.3 us
    transpose x0 -> x1, local copies, waits for them, and re-layouts: none -> 1.64 us  [local(): return jnp.transpose(out, (2, 0, 1))]
    add x2 -> x0, other arithmetic: 1.16 us -> none  [the longest x1 1.08 us: local(): return denominator * amplitudes.astype(F32) + ladder]
    pallas_call x1, Pallas kernels: 72.4 us -> 71.3 us  [local(): pl.pallas_call(kernel, out_shape=jax.ShapeDtypeStruct((pairs, cols, rows)...]
    dynamic_slice x1 -> x0, local copies, waits for them, and re-layouts: 0.83 us -> none  [local(): lax.dynamic_slice_in_dim(virt_energy, lax.axis_index('blk') * rows, rows)]
where the time goes in v3:
time: 73.1 us; the launch traced here: 73 us
  Pallas kernels  71.3 us (98%)
  local copies, waits for them, and re-layouts  1.64 us (2%)
    pallas_call x1, Pallas kernels, local(): pl.pallas_call(kernel, out_shape=jax.ShapeDtypeStruct((pairs, cols, rows)...  71.3 us
    transpose x1, local copies, waits for them, and re-layouts, local(): return jnp.transpose(out, (2, 0, 1))  1.64 us

profile of v3, /device:TPU:1, one launch (start us, length us, event | category | flops | bytes accessed | tf_op | source)
XLA Modules:
  0.0 73.0 jit_solution(9649710997130365523)
XLA Ops:
  0.0 71.3 %shard_map.55 = f32[4,56,56]{2,1,0:T(8,128)} custom-call(bf16[56,4,56]{2,1,0:T(4,128)(2,1)} %amp_hbm.1, bf16[32,896]{1,0:T(8,128)(2,1)} %x_hbm.1, f32[512,1,512]{2,1,0:T(1,128)} %z_hbm.1, f32[7,128]{1,0:T(8,128)} %bitcast.3, f32[4]{0:T(128)} %pe_hbm.1), custom_call_target="tpu_custom_call" | custom-call | tf_op jit(solution)/shard_map/pallas_call | solution.py:413
  71.3 1.6 %copy.6 = f32[56,4,56]{2,1,0:T(4,128)} copy(f32[56,4,56]{0,2,1:T(8,128)} %bitcast.2) | data formatting | bytes 100352 | tf_op jit(solution)/shard_map/transpose | solution.py:457

commit v4 on v3

--- a/solution.py
+++ b/solution.py
@@ -10,36 +10,40 @@
 MESH = pl.DeviceIdType.MESH
 F32 = jnp.float32
 BF16 = jnp.bfloat16
-SEMS = 200
+NAMES, KINDS = 89, 15
 
 
 class Links:
     def __init__(self, send, recv):
-        self.send, self.recv, self.ids, self.open = send, recv, {}, []
-
-    def index(self, key):
-        assert len(self.ids) < SEMS
-        return self.ids.setdefault(key, len(self.ids))
-
-    def copy(self, key, src, dst, dev):
-        i = self.index(key)
+        self.send, self.recv, self.ids, self.kinds = send, recv, {}, {}
+
+    def index(self, names, name, most):
+        assert name in names or len(names) < most
+        return names.setdefault(name, len(names))
+
+    def copy(self, kind, name, src, dst, dev):
         return pltpu.make_async_remote_copy(
-            src_ref=src, dst_ref=dst, send_sem=self.send.at[i], recv_sem=self.recv.at[i],
+            src_ref=src, dst_ref=dst,
+            send_sem=self.send.at[self.index(self.kinds, kind, KINDS)],
+            recv_sem=self.recv.at[self.index(self.ids, name, NAMES)],
             device_id=dev, device_id_type=MESH,
         )
 
-    def start(self, key, src, dst, dev):
-        c = self.copy(key, src, dst, dev)
-        c.start()
-        self.open.append(c)
-
-    def arrived(self, key, dst, dev):
-        self.copy(key, dst, dst, dev).wait_recv()
-
-    def close(self):
-        for c in self.open:
-            c.wait_send()
-        self.open = []
+    def start(self, kind, name, src, dst, dev):
+        self.copy(kind, name, src, dst, dev).start()
+
+    def arrived(self, name, dst, dev):
+        i = self.index(self.ids, name, NAMES)
+        pltpu.make_async_remote_copy(
+            src_ref=dst, dst_ref=dst, send_sem=self.send.at[0], recv_sem=self.recv.at[i],
+            device_id=dev, device_id_type=MESH,
+        ).wait_recv()
+
+    def sent(self, kind, all_of_them, dev):
+        pltpu.make_async_remote_copy(
+            src_ref=all_of_them, dst_ref=all_of_them, send_sem=self.send.at[self.kinds[kind]],
+            recv_sem=self.recv.at[0], device_id=dev, device_id_type=MESH,
+        ).wait_send()
 
 
 def kernel(
@@ -66,7 +70,7 @@
             "grp": ((1 - yl) if dyl else yl) * 8 + (z + dz) % 8,
         }
 
-    mate, yp = at(0, 0, 1), at(0, 1)
+    mate, xn, yp = at(0, 0, 1), at(1, 0), at(0, 1)
     zn, zv, yn = up(1), up(7), up(0, 1)
     around = [(2, 1), (3, 1), (1, 1), (2, 0), (3, 0), (1, 0)]
 
@@ -115,29 +119,29 @@
     far = (4, 3, 5, 2, 6, 1, 7)
 
     def t_send(k):
-        net.start(("t", k, 0, 1), tt_ref.at[2 * (1 - core) + k], tall.at[k, core, g], mate)
+        net.start("t", ("t", k, 0), tt_ref.at[2 * (1 - core) + k], tall.at[k, core, g], mate)
         for dz in far:
             for dc in range(2):
                 pair = 2 * ((1 - core) if dc else core) + k
-                net.start(("t", k, dz, dc), tt_ref.at[pair], tall.at[k, core, g], up(dz, 0, dc))
+                net.start("t", ("t", k, dz), tt_ref.at[pair], tall.at[k, core, g], up(dz, 0, dc))
         tall[k, core, g] = tt_ref[2 * core + k]
 
     def t_forward(k, dz):
         j = gi(-dz, 0)
-        for dc in range(2):
-            if dz or dc:
-                part = tall.at[k, (1 - core) if dc else core, j]
-                net.arrived(("t", k, dz, dc), part, up(8 - dz, 0, dc))
-        net.start(("ty", k, dz), tall.at[k, :, j], tall.at[k, :, j], yn)
+        if dz:
+            net.arrived(("t", k, dz), tall.at[k, :, j], up(8 - dz))
+        else:
+            net.arrived(("t", k, dz), tall.at[k, 1 - core, j], mate)
+        net.start("ty", ("ty", k), tall.at[k, :, j], tall.at[k, :, j], yn)
 
     t_send(0)
-    net.start("xpy", x_ref, xpa(0, 0), yn)
+    net.start("x", "xpy", x_ref, xpa(0, 0), yn)
     for dx, dy in ((0, 1), (1, 0), (3, 0), (2, 0)):
-        net.start(("xq", dx, dy), x_ref, xqa(0, 0), at(dx, dy))
-    net.start(("xqm", 0, 0), x_ref, xqa(0, 0), mate)
-    net.start(("xpn", 0, 1), x_ref, xpa(0, 0), zn)
-    net.start(("xpv", 0, 1), x_ref, xpa(0, 0), zv)
-    net.start(("xpm", 0, 0), x_ref, xpa(0, 0), mate)
+        net.start("x", ("xq", dx, dy), x_ref, xqa(0, 0), at(dx, dy))
+    net.start("x", "xqm", x_ref, xqa(0, 0), mate)
+    net.start("xp", ("xpn", 0, 1), x_ref, xpa(0, 0), zn)
+    net.start("xp", ("xpv", 0, 1), x_ref, xpa(0, 0), zv)
+    net.start("xpm", "xpm", x_ref, xpa(0, 0), mate)
     xq[m, core] = x_ref[...]
     xp[core, g] = x_ref[...]
 
@@ -146,14 +150,13 @@
         net.arrived(("xq", dx, dy), part, at(4 - dx, 0 if dx else dy))
         if (dx, dy) == (0, 1):
             for to in (1, 3, 2):
-                net.start(("xq", to, 1), part, part, at(to, 0))
-        net.start(("xqm", dx, dy), part, part, mate)
+                net.start("x", ("xq", to, 1), part, part, at(to, 0))
+        net.start("x", "xqm", part, part, mate)
 
     lane = lax.broadcasted_iota(jnp.int32, (512, 128), 1)
 
     def first(k):
-        for dz in (0,) + far:
-            net.arrived(("ty", k, dz), tall.at[k, :, gi(-dz, 1)], yn)
+        net.arrived(("ty", k), tall.at[k, :, pl.ds(8 * (1 - yl), 8)], yn)
         one = tall[k, 0].reshape(512, 128).astype(F32)
         two = tall[k, 1].reshape(512, 128).astype(F32)
         top = jnp.where(lane < 64, one, pltpu.roll(two, 64, 1))
@@ -168,18 +171,18 @@
         )
         right[k, rows(0, 0)] = jnp.concatenate([rt[:56], rt[64:120]], axis=0).astype(BF16)
         own = right.at[k, rows(0, 0)]
-        net.start(("ry", k, 0), own, own, yp)
+        net.start("r", ("ry", k), own, own, yp)
         for dx in (1, 3, 2):
-            net.start(("rx", k, dx), own, own, at(dx, 0))
+            net.start("r", ("rx", k, dx), own, own, at(dx, 0))
 
     def xp_mate(dyl, dz):
-        net.start(("xpm", dyl, dz), xpa(dyl, dz), xpa(dyl, dz), mate)
+        net.start("xpm", "xpm", xpa(dyl, dz), xpa(dyl, dz), mate)
 
     def xp_y():
         part = xpa(1, 0)
         net.arrived("xpy", part, yn)
-        net.start(("xpn", 1, 1), part, part, zn)
-        net.start(("xpv", 1, 1), part, part, zv)
+        net.start("xp", ("xpn", 1, 1), part, part, zn)
+        net.start("xp", ("xpv", 1, 1), part, part, zv)
         xp_mate(1, 0)
 
     def xp_step(s, dyl):
@@ -187,32 +190,30 @@
             part = xpa(dyl, -s)
             net.arrived(("xpn", dyl, s), part, zv)
             if s < 3 or (s == 3 and dyl == 0):
-                net.start(("xpn", dyl, s + 1), part, part, zn)
+                net.start("xp", ("xpn", dyl, s + 1), part, part, zn)
             xp_mate(dyl, -s)
         if s < 4 or dyl == 1:
             part = xpa(dyl, s)
             net.arrived(("xpv", dyl, s), part, zn)
             if s < 3 or (s == 3 and dyl == 1):
-                net.start(("xpv", dyl, s + 1), part, part, zv)
+                net.start("xp", ("xpv", dyl, s + 1), part, part, zv)
             xp_mate(dyl, s)
 
     def r_y(k):
-        net.arrived(("ry", k, 0), right.at[k, rows(0, 1)], yp)
+        net.arrived(("ry", k), right.at[k, rows(0, 1)], yp)
         part = right.at[k, rows(0, 1, 0, 48)]
         for dx in (1, 3, 2):
-            net.start(("rz", k, dx), part, part, at(dx, 0))
+            net.start("r2", ("rz", k), part, part, at(dx, 0))
 
     def r_x(k, *ways):
         for dx in ways:
             net.arrived(("rx", k, dx), right.at[k, rows(-dx, 0)], at(4 - dx, 0))
             part = right.at[k, rows(-dx, 0, 48, 64)]
-            net.start(("ry", k, dx), part, part, yp)
+            net.start("r2", ("rw", k), part, part, yp)
 
     def r_last(k):
-        for dx in (1, 3, 2):
-            net.arrived(("rz", k, dx), right.at[k, rows(-dx, 1, 0, 48)], at(4 - dx, 0))
-        for dx in (1, 3, 2):
-            net.arrived(("ry", k, dx), right.at[k, rows(-dx, 1, 48, 64)], yp)
+        net.arrived(("rz", k), right.at[k, pl.ds(0, 144)], xn)
+        net.arrived(("rw", k), right.at[k, pl.ds(0, 192)], yp)
 
     def weigh(k, c):
         p = jnp.dot(xp[c].reshape(512, 896), right[k], preferred_element_type=F32)
@@ -227,11 +228,11 @@
     def e_start(k):
         for i, dx in enumerate(order):
             eys[k, i] = mp[k, rows(dx, 1, 48, 64), :].astype(BF16)
-            net.start(("ey", k, dx), eys.at[k, i], eyr.at[k, i], yp)
+            net.start("ey", ("ey", k, dx), eys.at[k, i], eyr.at[k, i], yp)
             if dx:
                 for o in range(2):
                     e1s[k, i, o] = mp[k, rows(dx, o, 0, 48), :].astype(BF16)
-                net.start(("e1", k, dx), e1s.at[k, i], e1r.at[k, i], at(dx, 0))
+                net.start("e1", ("e1", k), e1s.at[k, i], e1r.at[k, i], at(dx, 0))
 
     def e_y(k, dx):
         i = order.index(dx)
@@ -241,20 +242,20 @@
     def e_two(k):
         for i, dx in enumerate(order[:3]):
             e2s[k, i] = e_y(k, dx).astype(BF16)
-            net.start(("e2", k, dx), e2s.at[k, i], e2r.at[k, i], at(dx, 0))
+            net.start("e2", ("e2", k), e2s.at[k, i], e2r.at[k, i], at(dx, 0))
 
     def e_three(k):
         v = mp[k, rows(0, 1, 0, 48), :]
-        for i, dx in enumerate(order[:3]):
-            net.arrived(("e1", k, dx), e1r.at[k, i], at(4 - dx, 0))
+        net.arrived(("e1", k), e1r.at[k], xn)
+        for i in range(3):
             v = v + e1r[k, i, 1].astype(F32)
         e3s[k] = v.astype(BF16)
-        net.start(("e3", k), e3s.at[k], e3r.at[k], yp)
+        net.start("e3", ("e3", k), e3s.at[k], e3r.at[k], yp)
 
     def e_last(k):
         v = e_y(k, 0)
-        for i, dx in enumerate(order[:3]):
-            net.arrived(("e2", k, dx), e2r.at[k, i], at(4 - dx, 0))
+        net.arrived(("e2", k), e2r.at[k], xn)
+        for i in range(3):
             v = v + e2r[k, i].astype(F32)
         u = mp[k, rows(0, 0, 0, 48), :]
         for i in range(3):
@@ -274,7 +275,7 @@
             v = lad[k, pl.ds(pl.multiple_of(j * 56, 8), 56), :]
             fs[k, j] = jnp.concatenate([v, gap], axis=0).astype(BF16)
         for dz in far + (0,):
-            net.start(("fy", k, dz), fs.at[k, gi(dz, 1)], fy.at[k, dz], yn)
+            net.start("fy", ("fy", k, dz), fs.at[k, gi(dz, 1)], fy.at[k, dz], yn)
 
     def fold(k):
         for dz in far + (0,):
@@ -284,7 +285,7 @@
             v = jnp.concatenate([v, jnp.zeros((8, 128), F32)], axis=0)
             if dz:
                 fs[k, j] = v.astype(BF16)
-                net.start(("f", k, dz), fs.at[k, j], fr.at[k, dz], up(dz))
+                net.start("f", ("f", k), fs.at[k, j], fr.at[k, dz], up(dz))
             else:
                 fins[k] = v
 
@@ -307,9 +308,7 @@
         for dx, dy in around[2::-1]:
             xq_forward(dx, dy)
     with jax.named_scope("xqm_wait"):
-        for dx, dy in around + [(0, 1), (0, 0)]:
-            part = xq.at[((x - dx + 4) % 4) * 2 + ((1 - yh) if dy else yh), 1 - core]
-            net.arrived(("xqm", dx, dy), part, mate)
+        net.arrived("xqm", xq.at[:, 1 - core], mate)
     scoped("first0", first, 0)
     scoped("xp_step20", xp_step, 2, 0)
     scoped("xp_step21", xp_step, 2, 1)
@@ -332,7 +331,7 @@
         both = second_e + first_e
         for k in range(4):
             base[k] = (both - pe[k]) * own_amp[k]
-    net.start("zsw", z_hbm.at[:, 0, :], zb.at[core], mate)
+    net.start("z", "z", z_hbm.at[:, 0, :], zb.at[core], mate)
     with jax.named_scope("t1"):
         for dz in (0,) + far[::-1]:
             t_forward(1, dz)
@@ -347,12 +346,9 @@
     scoped("xp_step41", xp_step, 4, 1)
     with jax.named_scope("z_wait"):
         zcopy.wait()
-        net.arrived("zsw", zb.at[1 - core], mate)
+        net.arrived("z", zb.at[1 - core], mate)
     with jax.named_scope("xpm_wait"):
-        for s in range(-4, 5):
-            for dyl in range(2):
-                if (s, dyl) not in ((4, 0), (-4, 1)):
-                    net.arrived(("xpm", dyl, s), xp.at[1 - core, gi(s, dyl)], mate)
+        net.arrived("xpm", xp.at[1 - core], mate)
     with jax.named_scope("xpt"):
         for t in range(4):
             xpt[:, 256 * t : 256 * t + 256] = jnp.transpose(
@@ -384,15 +380,14 @@
     scoped("ladder1", ladder, 1, v1)
     scoped("fold0", fold, 0)
     scoped("fold1", fold, 1)
-    scoped("close1", net.close)
     for k in range(2):
         total = fins[k]
         with jax.named_scope(f"f_wait{k}"):
+            net.arrived(("f", k), fr.at[k, pl.ds(1, 7)], zn)
             for dz in far:
-                net.arrived(("f", k, dz), fr.at[k, dz], up(8 - dz))
                 total = total + fr[k, dz].astype(F32)
         fins[k] = total
-        net.start(("fin", k), fins.at[k], finr.at[k], mate)
+        net.start("fin", ("fin", k), fins.at[k], finr.at[k], mate)
     def finish(pair, v):
         v = jnp.where(core == 0, v[:56, :64], v[:56, 64:]) + base[pair]
         out_ref[pair] = v[:, :56]
@@ -404,7 +399,13 @@
             net.arrived(("fin", k), finr.at[k], mate)
             finish(2 * (1 - core) + k, finr[k])
     with jax.named_scope("close"):
-        net.close()
+        for kind, whole in (
+            ("t", tall.at[:, 0, pl.ds(0, 15)]), ("ty", tall.at[:, 0]), ("x", xq),
+            ("xp", xp.at[0, pl.ds(0, 14)]), ("xpm", xp.at[0]), ("z", zb.at[0]),
+            ("r", right.at[0]), ("r2", right.at[0, pl.ds(0, 672)]), ("ey", eys), ("e1", e1s),
+            ("e2", e2s), ("e3", e3s), ("fy", fy), ("f", fr.at[:, pl.ds(0, 7)]), ("fin", fins),
+        ):
+            net.sent(kind, whole, mate)
 
 
 def local(amplitudes, grid_factor, metric, virt_energy, pair_energy):
@@ -412,7 +413,7 @@
     hbm = pl.BlockSpec(memory_space=pltpu.HBM)
     out = pl.pallas_call(
         kernel,
-        out_shape=jax.ShapeDtypeStruct((pairs, cols, rows), F32),
+        out_shape=pltpu.VMEM((pairs, cols, rows), F32),
         in_specs=[hbm] * 5,
         out_specs=pl.BlockSpec(memory_space=pltpu.VMEM),
         scratch_shapes=[
@@ -446,8 +447,8 @@
             pltpu.VMEM((2, 8, 64, 128), BF16),
             pltpu.VMEM((2, 64, 128), F32),
             pltpu.VMEM((2, 64, 128), F32),
-            pltpu.SemaphoreType.DMA((SEMS,)),
-            pltpu.SemaphoreType.DMA((SEMS,)),
+            pltpu.SemaphoreType.DMA((KINDS,)),
+            pltpu.SemaphoreType.DMA((NAMES,)),
             pltpu.SemaphoreType.DMA((5,)),
         ],
         compiler_params=pltpu.CompilerParams(

time: 73.1 us -> 68.8 us (0.941)
  Pallas kernels: 71.3 us -> 68 us
  local copies, waits for them, and re-layouts: 1.64 us -> 0.74 us
    pallas_call x1, Pallas kernels: 71.3 us -> 68 us  [local(): pl.pallas_call(kernel, out_shape=pltpu.VMEM((pairs, cols, rows), F32), in...]
    transpose x1, local copies, waits for them, and re-layouts: 1.64 us -> 0.74 us  [local(): return jnp.transpose(out, (2, 0, 1))]
where the time goes in v4:
time: 68.8 us; the launch traced here: 68.7 us
  Pallas kernels  68 us (99%)
  local copies, waits for them, and re-layouts  0.74 us (1%)
    pallas_call x1, Pallas kernels, local(): pl.pallas_call(kernel, out_shape=pltpu.VMEM((pairs, cols, rows), F32), in...  68 us

profile of v4, /device:TPU:1, one launch (start us, length us, event | category | flops | bytes accessed | tf_op | source)
XLA Modules:
  0.0 68.7 jit_solution(6200900552206638765)
XLA Ops:
  0.0 68.0 %shard_map.55 = f32[4,56,56]{2,1,0:T(8,128)S(1)} custom-call(bf16[56,4,56]{2,1,0:T(4,128)(2,1)} %amp_hbm.1, bf16[32,896]{1,0:T(8,128)(2,1)} %x_hbm.1, f32[512,1,512]{2,1,0:T(1,128)} %z_hbm.1, f32[7,128]{1,0:T(8,128)} %bitcast.3, f32[4]{0:T(128)} %pe_hbm.1), custom_call_target="tpu_custom_call" | custom-call | tf_op jit(solution)/shard_map/pallas_call | solution.py:414
  68.0 0.7 %copy.6 = f32[56,4,56]{2,1,0:T(4,128)} copy(f32[56,4,56]{0,2,1:T(8,128)S(1)} %bitcast.2) | data formatting | bytes 100352 | tf_op jit(solution)/shard_map/transpose | solution.py:458

commit v5 on v4

--- a/solution.py
+++ b/solution.py
@@ -10,7 +10,7 @@
 MESH = pl.DeviceIdType.MESH
 F32 = jnp.float32
 BF16 = jnp.bfloat16
-NAMES, KINDS = 89, 15
+NAMES, KINDS = 90, 15
 
 
 class Links:
@@ -79,7 +79,7 @@
         return pl.ds(pl.multiple_of((((x + dx + 4) % 4) * 2 + yy) * 112 + first, 16), count)
 
     def xqa(dx, dy):
-        return xq.at[((x + dx + 4) % 4) * 2 + ((1 - yh) if dy else yh), core]
+        return xq.at[(1 - yh) if dy else yh, (x + dx + 4) % 4, core]
 
     def gi(dz, dyl):
         return ((1 - yl) if dyl else yl) * 8 + (z + dz + 8) % 8
@@ -138,11 +138,11 @@
     net.start("x", "xpy", x_ref, xpa(0, 0), yn)
     for dx, dy in ((0, 1), (1, 0), (3, 0), (2, 0)):
         net.start("x", ("xq", dx, dy), x_ref, xqa(0, 0), at(dx, dy))
-    net.start("x", "xqm", x_ref, xqa(0, 0), mate)
+    net.start("x", ("xqm", 0), x_ref, xqa(0, 0), mate)
     net.start("xp", ("xpn", 0, 1), x_ref, xpa(0, 0), zn)
     net.start("xp", ("xpv", 0, 1), x_ref, xpa(0, 0), zv)
     net.start("xpm", "xpm", x_ref, xpa(0, 0), mate)
-    xq[m, core] = x_ref[...]
+    xq[yh, x, core] = x_ref[...]
     xp[core, g] = x_ref[...]
 
     def xq_forward(dx, dy):
@@ -151,11 +151,11 @@
         if (dx, dy) == (0, 1):
             for to in (1, 3, 2):
                 net.start("x", ("xq", to, 1), part, part, at(to, 0))
-        net.start("x", "xqm", part, part, mate)
+        net.start("x", ("xqm", dy), part, part, mate)
 
     lane = lax.broadcasted_iota(jnp.int32, (512, 128), 1)
 
-    def first(k):
+    def gathered(k):
         net.arrived(("ty", k), tall.at[k, :, pl.ds(8 * (1 - yl), 8)], yn)
         one = tall[k, 0].reshape(512, 128).astype(F32)
         two = tall[k, 1].reshape(512, 128).astype(F32)
@@ -165,15 +165,25 @@
             [v for j in range(16) for v in (top[32 * j : 32 * j + 32], low[32 * j : 32 * j + 24])],
             axis=0,
         )
+        return t.astype(BF16)
+
+    def first(k, t, half):
         rt = lax.dot_general(
-            t.astype(BF16), xq[...].reshape(512, 896), (((0,), (1,)), ((), ())),
-            preferred_element_type=F32,
+            t, xq[half].reshape(256, 896), (((0,), (1,)), ((), ())), preferred_element_type=F32
         )
-        right[k, rows(0, 0)] = jnp.concatenate([rt[:56], rt[64:120]], axis=0).astype(BF16)
-        own = right.at[k, rows(0, 0)]
-        net.start("r", ("ry", k), own, own, yp)
+        cols = pl.ds(pl.multiple_of(half * 256, 256), 256)
+        rt = jnp.concatenate([rt[:56], rt[64:120]], axis=0)
+        right[k, rows(0, 0), cols] = rt.astype(BF16)
+        return cols
+
+    def r_send(k, cols):
+        head, tail = right.at[k, rows(0, 0, 0, 64), cols], right.at[k, rows(0, 0, 64, 48), cols]
+        net.start("r", ("ry", k), head, head, yp)
         for dx in (1, 3, 2):
-            net.start("r", ("rx", k, dx), own, own, at(dx, 0))
+            net.start("r", ("rx", k, dx), tail, tail, at(dx, 0))
+        net.start("r", ("rw", k), tail, tail, yp)
+        for dx in (1, 3, 2):
+            net.start("r", ("rz", k), head, head, at(dx, 0))
 
     def xp_mate(dyl, dz):
         net.start("xpm", "xpm", xpa(dyl, dz), xpa(dyl, dz), mate)
@@ -200,19 +210,19 @@
             xp_mate(dyl, s)
 
     def r_y(k):
-        net.arrived(("ry", k), right.at[k, rows(0, 1)], yp)
-        part = right.at[k, rows(0, 1, 0, 48)]
+        net.arrived(("ry", k), right.at[k, rows(0, 1, 0, 64)], yp)
+        part = right.at[k, rows(0, 1, 0, 64)]
         for dx in (1, 3, 2):
             net.start("r2", ("rz", k), part, part, at(dx, 0))
 
     def r_x(k, *ways):
         for dx in ways:
-            net.arrived(("rx", k, dx), right.at[k, rows(-dx, 0)], at(4 - dx, 0))
-            part = right.at[k, rows(-dx, 0, 48, 64)]
+            net.arrived(("rx", k, dx), right.at[k, rows(-dx, 0, 64, 48)], at(4 - dx, 0))
+            part = right.at[k, rows(-dx, 0, 64, 48)]
             net.start("r2", ("rw", k), part, part, yp)
 
     def r_last(k):
-        net.arrived(("rz", k), right.at[k, pl.ds(0, 144)], xn)
+        net.arrived(("rz", k), right.at[k, pl.ds(0, 384)], xn)
         net.arrived(("rw", k), right.at[k, pl.ds(0, 192)], yp)
 
     def weigh(k, c):
@@ -304,12 +314,16 @@
     scoped("xp_step10", xp_step, 1, 0)
     scoped("xp_step11", xp_step, 1, 1)
     t_send(1)
+    with jax.named_scope("first0a"):
+        net.arrived(("xqm", 0), xq.at[yh, :, 1 - core], mate)
+        t0 = gathered(0)
+        r_send(0, first(0, t0, yh))
     with jax.named_scope("xq_far"):
         for dx, dy in around[2::-1]:
             xq_forward(dx, dy)
-    with jax.named_scope("xqm_wait"):
-        net.arrived("xqm", xq.at[:, 1 - core], mate)
-    scoped("first0", first, 0)
+        net.arrived(("xqm", 1), xq.at[1 - yh, :, 1 - core], mate)
+    with jax.named_scope("first0"):
+        r_send(0, first(0, t0, 1 - yh))
     scoped("xp_step20", xp_step, 2, 0)
     scoped("xp_step21", xp_step, 2, 1)
     with jax.named_scope("xqt"):
@@ -331,7 +345,22 @@
         both = second_e + first_e
         for k in range(4):
             base[k] = (both - pe[k]) * own_amp[k]
-    net.start("z", "z", z_hbm.at[:, 0, :], zb.at[core], mate)
+    with jax.named_scope("z_order"):
+        zcopy.wait()
+
+        def swap(i, carry):
+            block = pl.ds(pl.multiple_of(64 * i, 64), 64)
+            v = [zb[core, block, 128 * c : 128 * c + 128] for c in range(4)]
+            u = [pltpu.roll(c, 64, 1) for c in v]
+            low = lax.broadcasted_iota(jnp.int32, (64, 128), 1) < 64
+            zb[core, block, 0:128] = jnp.where(low, v[0], u[1])
+            zb[core, block, 128:256] = jnp.where(low, v[2], u[3])
+            zb[core, block, 256:384] = jnp.where(low, u[0], v[1])
+            zb[core, block, 384:512] = jnp.where(low, u[2], v[3])
+            return carry
+
+        lax.fori_loop(0, 8, swap, 0)
+    net.start("z", "z", zb.at[core], zb.at[core], mate)
     with jax.named_scope("t1"):
         for dz in (0,) + far[::-1]:
             t_forward(1, dz)
@@ -341,11 +370,14 @@
     scoped("xp_step31", xp_step, 3, 1)
     scoped("r_y0", r_y, 0)
     scoped("r_x02", r_x, 0, 2)
-    scoped("first1", first, 1)
+    with jax.named_scope("first1"):
+        t1 = gathered(1)
+        for half in range(2):
+            first(1, t1, half)
+        r_send(1, pl.ds(0, 512))
     scoped("xp_step40", xp_step, 4, 0)
     scoped("xp_step41", xp_step, 4, 1)
     with jax.named_scope("z_wait"):
-        zcopy.wait()
         net.arrived("z", zb.at[1 - core], mate)
     with jax.named_scope("xpm_wait"):
         net.arrived("xpm", xp.at[1 - core], mate)
@@ -425,7 +457,7 @@
             pltpu.VMEM((4, 56, 64), F32),
             pltpu.VMEM((4, 56, 64), F32),
             pltpu.VMEM((2, 2, 16, 32, 128), BF16),
-            pltpu.VMEM((8, 2, 32, 896), BF16),
+            pltpu.VMEM((2, 4, 2, 32, 896), BF16),
             pltpu.VMEM((896, 512), BF16),
             pltpu.VMEM((2, 16, 32, 896), BF16),
             pltpu.VMEM((896, 1024), BF16),

time: 68.8 us -> 67.3 us (0.978)
  Pallas kernels: 68 us -> 66.4 us
    pallas_call x1, Pallas kernels: 68 us -> 66.4 us  [local(): pl.pallas_call(kernel, out_shape=pltpu.VMEM((pairs, cols, rows), F32), in...]
where the time goes in v5:
time: 67.3 us; the launch traced here: 67.2 us
  Pallas kernels  66.4 us (99%)
  local copies, waits for them, and re-layouts  0.74 us (1%)
    pallas_call x1, Pallas kernels, local(): pl.pallas_call(kernel, out_shape=pltpu.VMEM((pairs, cols, rows), F32), in...  66.4 us

profile of v5, /device:TPU:1, one launch (start us, length us, event | category | flops | bytes accessed | tf_op | source)
XLA Modules:
  0.0 67.2 jit_solution(4183282014197170864)
XLA Ops:
  0.0 66.4 %shard_map.55 = f32[4,56,56]{2,1,0:T(8,128)S(1)} custom-call(bf16[56,4,56]{2,1,0:T(4,128)(2,1)} %amp_hbm.1, bf16[32,896]{1,0:T(8,128)(2,1)} %x_hbm.1, f32[512,1,512]{2,1,0:T(1,128)} %z_hbm.1, f32[7,128]{1,0:T(8,128)} %bitcast.3, f32[4]{0:T(128)} %pe_hbm.1), custom_call_target="tpu_custom_call" | custom-call | tf_op jit(solution)/shard_map/pallas_call | solution.py:446
  66.4 0.7 %copy.6 = f32[56,4,56]{2,1,0:T(4,128)} copy(f32[56,4,56]{0,2,1:T(8,128)S(1)} %bitcast.2) | data formatting | bytes 100352 | tf_op jit(solution)/shard_map/transpose | solution.py:490

commit v6 on v5

--- a/solution.py
+++ b/solution.py
@@ -116,11 +116,11 @@
         xcopy.wait()
         pl.semaphore_wait(barrier, len(near))
 
-    far = (4, 3, 5, 2, 6, 1, 7)
+    far, mixed = (4, 3, 5, 2, 6, 1, 7), (4, 1, 7, 3, 5, 2, 6)
 
     def t_send(k):
         net.start("t", ("t", k, 0), tt_ref.at[2 * (1 - core) + k], tall.at[k, core, g], mate)
-        for dz in far:
+        for dz in mixed:
             for dc in range(2):
                 pair = 2 * ((1 - core) if dc else core) + k
                 net.start("t", ("t", k, dz), tt_ref.at[pair], tall.at[k, core, g], up(dz, 0, dc))
@@ -276,23 +276,23 @@
     def ladder(k, v):
         gap = jnp.zeros((8, 512), F32)
         v = jnp.concatenate([v[:56], gap, v[56:], gap], axis=0).astype(BF16)
-        lad[k] = lax.dot_general(
-            xqt[...], v, (((1,), (1,)), ((), ())), preferred_element_type=F32
-        )
-        gap = jnp.zeros((8, 128), F32)
-        for dz in range(8):
-            j = gi(dz, 1)
-            v = lad[k, pl.ds(pl.multiple_of(j * 56, 8), 56), :]
-            fs[k, j] = jnp.concatenate([v, gap], axis=0).astype(BF16)
-        for dz in far + (0,):
-            net.start("fy", ("fy", k, dz), fs.at[k, gi(dz, 1)], fy.at[k, dz], yn)
+        for column in (1 - yl, yl):
+            part = pl.ds(pl.multiple_of(column * 448, 64), 448)
+            lad[k, part] = lax.dot_general(
+                xqt[part, :], v, (((1,), (1,)), ((), ())), preferred_element_type=F32
+            )
+            if column is not yl:
+                for dz in far + (0,):
+                    j = gi(dz, 1)
+                    u = lad[k, pl.ds(pl.multiple_of(j * 56, 8), 56), :]
+                    fs[k, j] = u.astype(BF16)
+                    net.start("fy", ("fy", k, dz), fs.at[k, j], fy.at[k, dz], yn)
 
     def fold(k):
         for dz in far + (0,):
             j = gi(dz, 0)
             net.arrived(("fy", k, dz), fy.at[k, dz], yn)
-            v = lad[k, pl.ds(pl.multiple_of(j * 56, 8), 56), :] + fy[k, dz, 0:56].astype(F32)
-            v = jnp.concatenate([v, jnp.zeros((8, 128), F32)], axis=0)
+            v = lad[k, pl.ds(pl.multiple_of(j * 56, 8), 56), :] + fy[k, dz].astype(F32)
             if dz:
                 fs[k, j] = v.astype(BF16)
                 net.start("f", ("f", k), fs.at[k, j], fr.at[k, dz], up(dz))
@@ -303,17 +303,19 @@
         with jax.named_scope(name):
             return f(*args)
 
+    scoped("t00", t_forward, 0, 0)
     scoped("xp_y", xp_y)
+    scoped("t01", t_forward, 0, 1)
+    scoped("t07", t_forward, 0, 7)
     scoped("xq_y", xq_forward, 0, 1)
     with jax.named_scope("t0_xq"):
-        t_forward(0, 0)
-        for i, dz in enumerate(far[::-1]):
+        for i, dz in enumerate((4, 3, 5, 2, 6)):
             t_forward(0, dz)
             if i < 3:
                 xq_forward(*around[::-1][i])
+    t_send(1)
     scoped("xp_step10", xp_step, 1, 0)
     scoped("xp_step11", xp_step, 1, 1)
-    t_send(1)
     with jax.named_scope("first0a"):
         net.arrived(("xqm", 0), xq.at[yh, :, 1 - core], mate)
         t0 = gathered(0)
@@ -345,6 +347,9 @@
         both = second_e + first_e
         for k in range(4):
             base[k] = (both - pe[k]) * own_amp[k]
+    with jax.named_scope("t1"):
+        for dz in (0, 1, 7, 4, 3, 5, 2, 6):
+            t_forward(1, dz)
     with jax.named_scope("z_order"):
         zcopy.wait()
 
@@ -361,9 +366,6 @@
 
         lax.fori_loop(0, 8, swap, 0)
     net.start("z", "z", zb.at[core], zb.at[core], mate)
-    with jax.named_scope("t1"):
-        for dz in (0,) + far[::-1]:
-            t_forward(1, dz)
     scoped("r_x01", r_x, 0, 1)
     scoped("xp_step30", xp_step, 3, 0)
     scoped("r_x03", r_x, 0, 3)
@@ -421,7 +423,7 @@
         fins[k] = total
         net.start("fin", ("fin", k), fins.at[k], finr.at[k], mate)
     def finish(pair, v):
-        v = jnp.where(core == 0, v[:56, :64], v[:56, 64:]) + base[pair]
+        v = jnp.where(core == 0, v[:, :64], v[:, 64:]) + base[pair]
         out_ref[pair] = v[:, :56]
 
     for k in range(2):
@@ -474,11 +476,11 @@
             pltpu.VMEM((2, 4, 64, 512), BF16),
             pltpu.VMEM((2, 4, 64, 512), BF16),
             pltpu.VMEM((2, 896, 128), F32),
-            pltpu.VMEM((2, 16, 64, 128), BF16),
-            pltpu.VMEM((2, 8, 64, 128), BF16),
-            pltpu.VMEM((2, 8, 64, 128), BF16),
-            pltpu.VMEM((2, 64, 128), F32),
-            pltpu.VMEM((2, 64, 128), F32),
+            pltpu.VMEM((2, 16, 56, 128), BF16),
+            pltpu.VMEM((2, 8, 56, 128), BF16),
+            pltpu.VMEM((2, 8, 56, 128), BF16),
+            pltpu.VMEM((2, 56, 128), F32),
+            pltpu.VMEM((2, 56, 128), F32),
             pltpu.SemaphoreType.DMA((KINDS,)),
             pltpu.SemaphoreType.DMA((NAMES,)),
             pltpu.SemaphoreType.DMA((5,)),

time: 67.3 us -> 67.2 us (level)
  no operation moved by 1% of the time
where the time goes in v6:
time: 67.2 us; the launch traced here: 67.1 us
  Pallas kernels  66.3 us (99%)
  local copies, waits for them, and re-layouts  0.74 us (1%)
    pallas_call x1, Pallas kernels, local(): pl.pallas_call(kernel, out_shape=pltpu.VMEM((pairs, cols, rows), F32), in...  66.3 us

profile of v6, /device:TPU:1, one launch (start us, length us, event | category | flops | bytes accessed | tf_op | source)
XLA Modules:
  0.0 67.1 jit_solution(8192637621230381647)
XLA Ops:
  0.0 66.3 %shard_map.55 = f32[4,56,56]{2,1,0:T(8,128)S(1)} custom-call(bf16[56,4,56]{2,1,0:T(4,128)(2,1)} %amp_hbm.1, bf16[32,896]{1,0:T(8,128)(2,1)} %x_hbm.1, f32[512,1,512]{2,1,0:T(1,128)} %z_hbm.1, f32[7,128]{1,0:T(8,128)} %bitcast.3, f32[4]{0:T(128)} %pe_hbm.1), custom_call_target="tpu_custom_call" | custom-call | tf_op jit(solution)/shard_map/pallas_call | solution.py:448
  66.3 0.7 %copy.6 = f32[56,4,56]{2,1,0:T(4,128)} copy(f32[56,4,56]{0,2,1:T(8,128)S(1)} %bitcast.2) | data formatting | bytes 100352 | tf_op jit(solution)/shard_map/transpose | solution.py:492

commit v7 on v6

--- a/solution.py
+++ b/solution.py
@@ -101,18 +101,6 @@
             pl.semaphore_signal(barrier, inc=1, device_id=dev, device_id_type=MESH)
         vcopy, pcopy = fetch(2, ve_hbm, ve.at[pl.ds(0, 7)]), fetch(3, pe_hbm, pe)
         zcopy = fetch(4, z_hbm.at[:, 0, :], zb.at[core])
-        acopy.wait()
-        eye = (
-            lax.broadcasted_iota(jnp.int32, (56, 64), 0)
-            == lax.broadcasted_iota(jnp.int32, (56, 64), 1)
-        ).astype(BF16)
-        for k in range(4):
-            t = lax.dot_general(
-                amp[:, k, :], eye, (((0,), (0,)), ((), ())), preferred_element_type=F32
-            )
-            own_amp[k] = t
-            t = jnp.concatenate([t, jnp.zeros((8, 64), F32)], axis=0)
-            tt_ref[k] = jnp.concatenate([t[:32], t[32:]], axis=1).astype(BF16)
         xcopy.wait()
         pl.semaphore_wait(barrier, len(near))
 
@@ -134,11 +122,23 @@
             net.arrived(("t", k, dz), tall.at[k, 1 - core, j], mate)
         net.start("ty", ("ty", k), tall.at[k, :, j], tall.at[k, :, j], yn)
 
-    t_send(0)
     net.start("x", "xpy", x_ref, xpa(0, 0), yn)
     for dx, dy in ((0, 1), (1, 0), (3, 0), (2, 0)):
         net.start("x", ("xq", dx, dy), x_ref, xqa(0, 0), at(dx, dy))
     net.start("x", ("xqm", 0), x_ref, xqa(0, 0), mate)
+    acopy.wait()
+    eye = (
+        lax.broadcasted_iota(jnp.int32, (56, 64), 0)
+        == lax.broadcasted_iota(jnp.int32, (56, 64), 1)
+    ).astype(BF16)
+    for k in range(4):
+        t = lax.dot_general(
+            amp[:, k, :], eye, (((0,), (0,)), ((), ())), preferred_element_type=F32
+        )
+        own_amp[k] = t
+        t = jnp.concatenate([t, jnp.zeros((8, 64), F32)], axis=0)
+        tt_ref[k] = jnp.concatenate([t[:32], t[32:]], axis=1).astype(BF16)
+    t_send(0)
     net.start("xp", ("xpn", 0, 1), x_ref, xpa(0, 0), zn)
     net.start("xp", ("xpv", 0, 1), x_ref, xpa(0, 0), zv)
     net.start("xpm", "xpm", x_ref, xpa(0, 0), mate)

time: 67.2 us -> 67.5 us (level)
  no operation moved by 1% of the time
where the time goes in v7:
time: 67.5 us; the launch traced here: 67.4 us
  Pallas kernels  66.7 us (99%)
  local copies, waits for them, and re-layouts  0.74 us (1%)
    pallas_call x1, Pallas kernels, local(): pl.pallas_call(kernel, out_shape=pltpu.VMEM((pairs, cols, rows), F32), in...  66.7 us

profile of v7, /device:TPU:1, one launch (start us, length us, event | category | flops | bytes accessed | tf_op | source)
XLA Modules:
  0.0 67.4 jit_solution(3211156184619221986)
XLA Ops:
  0.0 66.7 %shard_map.55 = f32[4,56,56]{2,1,0:T(8,128)S(1)} custom-call(bf16[56,4,56]{2,1,0:T(4,128)(2,1)} %amp_hbm.1, bf16[32,896]{1,0:T(8,128)(2,1)} %x_hbm.1, f32[512,1,512]{2,1,0:T(1,128)} %z_hbm.1, f32[7,128]{1,0:T(8,128)} %bitcast.3, f32[4]{0:T(128)} %pe_hbm.1), custom_call_target="tpu_custom_call" | custom-call | tf_op jit(solution)/shard_map/pallas_call | solution.py:448
  66.7 0.7 %copy.6 = f32[56,4,56]{2,1,0:T(4,128)} copy(f32[56,4,56]{0,2,1:T(8,128)S(1)} %bitcast.2) | data formatting | bytes 100352 | tf_op jit(solution)/shard_map/transpose | solution.py:492
